TPU v7x, 128 devices: a whole 4x4x4 slice. The times are simulated.
128 devices in a mesh: orb: 64 (over x, z, y), trial: 2 (over core).
Axes of the slice: x: 4, y: 4, z: 4, core: 2. Of those that a mesh axis runs over, the one named last changes fastest.
Arguments:
- trials: float32 [4, 64, 4096], P('trial', 'orb'), may hold values from -120 to 120
- orbitals: bfloat16 [128, 64, 4096], P('orb'), may hold values from -6 to 6
- potential: float32 [64, 4096], P('orb'), may hold values from 0.5 to 2
- coulomb: float32 [3, 64, 64], replicated, may hold values from -0.75 to 0.75
- energies: float32 [128], replicated, may hold values from -1.5 to -0.3
- frequencies: float32 [8], replicated, may hold values from 0.3 to 4
- orbital_ids: int32 [128], P('orb'), may hold values from 0 to 127, each once
- freq_index: int32 [128], P('orb'), may hold values from 0 to 7
Outputs:
- filtered: float32 [4, 64, 4096], P('trial', 'orb')
All inputs are finite; a program needn't handle non-finite values.
Results may differ from a plain program's by a relative error of at most 0.0003.
Values sent between devices are 32-bit elements; how exact they have to be, the bound alone decides.
A program may use at most 64 MiB of HBM per device.

v0:
```python
import jax
import jax.numpy as jnp
from jax import lax
from jax.sharding import PartitionSpec as P

G = 64
ITERS = 3


def from_everyone(shard, axis):
    length = lax.axis_size(axis)
    return lax.all_to_all(
        jnp.broadcast_to(shard[None], (length, *shard.shape)), axis, 0, 0, tiled=True
    )


def in_order(tiles, dim):
    lengths = list(tiles.shape[1:])
    lengths[dim] *= tiles.shape[0]
    return jnp.moveaxis(tiles, 0, dim).reshape(lengths)


def gathered_copies(shard, axis, dim):
    tiles = from_everyone(shard, axis)
    return in_order(tiles, dim)


def split_up(shard, dim, length):
    before, after = (shard.shape[:dim], shard.shape[dim + 1 :])
    return jnp.moveaxis(shard.reshape(*before, length, -1, *after), dim, 0)


def sum_at_owner(shard, axis, dim):
    tiles = split_up(shard, dim, lax.axis_size(axis))
    arrived = lax.all_to_all(tiles, axis, split_axis=0, concat_axis=0, tiled=True)
    return arrived.sum(axis=0)


def over_copies(shard, axis):
    return from_everyone(shard, axis).sum(axis=0)


def packed_total(arrays, axis):
    ends = [0]
    for a in arrays:
        ends.append(ends[-1] + a.size)
    subtotal = over_copies(jnp.concatenate([a.ravel() for a in arrays]), axis)
    return tuple((subtotal[b:e].reshape(a.shape) for a, b, e in zip(arrays, ends, ends[1:])))


def orbital_shifts(orbital_ids, freq_index, energies, frequencies):
    energy_slots = lax.broadcasted_iota(jnp.int32, (1, energies.shape[0]), 1)
    picked_energy = jnp.sum(
        jnp.where(orbital_ids[:, None] == energy_slots, energies[None, :], 0.0), axis=1
    )
    freq_slots = lax.broadcasted_iota(jnp.int32, (1, frequencies.shape[0]), 1)
    picked_freq = jnp.sum(
        jnp.where(freq_index[:, None] == freq_slots, frequencies[None, :], 0.0), axis=1
    )
    return picked_freq - picked_energy


def neighbour_sum(grid_field):
    grid_width = grid_field.shape[-2]
    z_index = lax.broadcasted_iota(jnp.int32, (1, grid_field.shape[-1]), 1) % grid_width
    zero_cells = jnp.zeros_like(grid_field[..., :1])
    upper_z = jnp.where(
        z_index == grid_width - 1, 0.0, jnp.concatenate([grid_field[..., 1:], zero_cells], axis=-1)
    )
    lower_z = jnp.where(
        z_index == 0, 0.0, jnp.concatenate([zero_cells, grid_field[..., :-1]], axis=-1)
    )
    zero_line = jnp.zeros_like(grid_field[..., :grid_width])
    upper_y = jnp.concatenate([grid_field[..., grid_width:], zero_line], axis=-1)
    lower_y = jnp.concatenate([zero_line, grid_field[..., :-grid_width]], axis=-1)
    zero_plane = jnp.zeros_like(grid_field[..., :1, :])
    upper_x = jnp.concatenate([grid_field[..., 1:, :], zero_plane], axis=-2)
    lower_x = jnp.concatenate([zero_plane, grid_field[..., :-1, :]], axis=-2)
    return upper_z + lower_z + upper_y + lower_y + upper_x + lower_x


def apply_shifted(grid_field, potential, level_shift):
    return (3.0 + potential + level_shift) * grid_field - 0.5 * neighbour_sum(grid_field)


def cell_inner(left_field, right_field):
    return jnp.sum(left_field * right_field, axis=(1, 2))


def sternheimer(source, potential, level_shift):
    iterate = jnp.zeros_like(source)
    residual = source
    direction = source
    norm_now = cell_inner(residual, residual)[:, None, None]
    for sweep_index in range(ITERS):
        mapped = apply_shifted(direction, potential, level_shift)
        step_size = norm_now / cell_inner(direction, mapped)[:, None, None]
        iterate = iterate + step_size * direction
        residual = residual - step_size * mapped
        norm_next = cell_inner(residual, residual)[:, None, None]
        direction = residual + norm_next / norm_now * direction
        norm_now = norm_next
    return iterate


def orbital_response(whole, orbitals, potential, shifts):

    def one_orbital(accumulated, scanned):
        orbital, level_shift = scanned
        density = orbital.astype(jnp.float32)[None]
        solved = sternheimer(density * whole, potential, level_shift)
        return (accumulated - density * solved, None)

    result, unused = lax.scan(one_orbital, jnp.zeros_like(whole), (orbitals, shifts))
    return result


def coulomb_full(grid_field, factors):
    trial_count = grid_field.shape[0]
    grid_width = grid_field.shape[1]
    cube_view = grid_field.reshape(trial_count, grid_width, grid_width, grid_width)
    cube_view = jnp.einsum("cz,txyz->txyc", factors[2], cube_view, precision=lax.Precision.HIGHEST)
    cube_view = jnp.einsum("by,txyc->txbc", factors[1], cube_view, precision=lax.Precision.HIGHEST)
    cube_view = jnp.einsum("ax,txbc->tabc", factors[0], cube_view, precision=lax.Precision.HIGHEST)
    return cube_view.reshape(trial_count, grid_width, grid_width * grid_width)


def shards(trials, orbitals, potential, coulomb, energies, frequencies, orbital_ids, freq_index):
    shifts = orbital_shifts(orbital_ids, freq_index, energies, frequencies)
    full_potential = gathered_copies(potential, "orb", 0)

    def apply_kernel(planes):
        whole = gathered_copies(planes, "orb", 1)
        partial_value = orbital_response(whole, orbitals, full_potential, shifts)
        partial_value = coulomb_full(partial_value, coulomb)
        summed = sum_at_owner(partial_value, "orb", 1)
        return summed

    mapped = apply_kernel(trials)
    squares, cross_sum, mapped_squares = packed_total(
        (cell_inner(trials, trials), cell_inner(trials, mapped), cell_inner(mapped, mapped)), "orb"
    )
    center = (cross_sum / squares)[:, None, None]
    spread = jnp.sqrt(mapped_squares / squares)[:, None, None]
    first = (mapped - center * trials) / spread
    second_mapped = apply_kernel(first)
    second = 2.0 * (second_mapped - center * first) / spread - trials
    block = gathered_copies(second, "trial", 0)
    columns = block.reshape(block.shape[0], -1)
    local_gram = jnp.dot(columns, columns.T, precision=lax.Precision.HIGHEST)
    gram_matrix = over_copies(local_gram, "orb") / float(G**3)
    lower = jnp.linalg.cholesky(gram_matrix)
    identity = jnp.eye(gram_matrix.shape[0], dtype=gram_matrix.dtype)
    inverse = lax.linalg.triangular_solve(lower, identity, left_side=True, lower=True)
    trial_count = second.shape[0]
    own_rows = lax.dynamic_slice_in_dim(
        inverse, lax.axis_index("trial") * trial_count, trial_count, 0
    )
    result = jnp.dot(own_rows, columns, precision=lax.Precision.HIGHEST)
    return result.reshape(second.shape)


def solution(mesh):
    in_specs = (
        P("trial", "orb", None),
        P("orb", None, None),
        P("orb", None),
        P(),
        P(),
        P(),
        P("orb"),
        P("orb"),
    )
    out_specs = P("trial", "orb", None)
    return jax.shard_map(shards, mesh=mesh, in_specs=in_specs, out_specs=out_specs, check_vma=False)
```

profile of v0, /device:TPU:0, one launch (start us, length us, event | category | flops | bytes accessed | tf_op | source)
XLA Modules:
  0.0 426.2 jit_solution(7948322079337206984)
XLA Ops:
  2.7 11.5 %all-to-all-start.1 = ((f32[64,1,4096]{2,1,0:T(1,128)}), f32[64,1,4096]{2,1,0:T(1,128)S(1)}, u32[]{:S(2)}, u32[]{:S(2)}) async-start(f32[64,1,4096]{2,1,0:T(1,128)} %broadcast_in_dim.195), calls=%async_computation.1 | async-start | bytes 2097152 | tf_op jit(solution)/shard_map/all_to_all | solution.py:12
  14.3 18.5 %all-to-all-done.1 = f32[64,1,4096]{2,1,0:T(1,128)S(1)} async-done(((f32[64,1,4096]{2,1,0:T(1,128)}), f32[64,1,4096]{2,1,0:T(1,128)S(1)}, u32[]{:S(2)}, u32[]{:S(2)}) %all-to-all-start.1) | async-done | bytes 1048608 | tf_op jit(solution)/shard_map/all_to_all | solution.py:12
  35.2 5.0 %all-to-all-start = ((f32[64,2,1,4096]{3,1,2,0:T(2,128)}), f32[64,2,1,4096]{3,1,2,0:T(2,128)S(1)}, u32[]{:S(2)}, u32[]{:S(2)}) async-start(f32[64,2,1,4096]{3,1,2,0:T(2,128)} %broadcast_in_dim.193), calls=%async_computation | async-start | bytes 4194304 | tf_op jit(solution)/shard_map/all_to_all | solution.py:12
  42.3 26.3 %all-to-all-done = f32[64,2,1,4096]{3,1,2,0:T(2,128)S(1)} async-done(((f32[64,2,1,4096]{3,1,2,0:T(2,128)}), f32[64,2,1,4096]{3,1,2,0:T(2,128)S(1)}, u32[]{:S(2)}, u32[]{:S(2)}) %all-to-all-start) | async-done | bytes 2097184 | tf_op jit(solution)/shard_map/all_to_all | solution.py:12
  71.2 63.0 %while.26 = (s32[]{:T(128)}, f32[2,64,4096]{2,1,0:T(8,128)}, bf16[2,64,4096]{2,1,0:T(8,128)(2,1)}, f32[2,64,4096]{2,1,0:T(8,128)}, f32[64,4096]{1,0:T(8,128)}, /*index=5*/f32[2]{0:T(128)S(1)}, s32[]{:T(128)}, s32[]{:T(128)}) while((s32[]{:T(128)}, f32[2,64,4096]{2,1,0:T(8,128)}, bf16[2,64,4096]{2,1,0:T(8,128)(2,1)}, ...), condition=%wide.region_9.10_spmd.clone, body=%wide.region_2.9_spmd.clone.sunk | while | flops 34897920 | bytes 182869376 | solution.py:114
  129.1 5.0 %select_subtract_fusion.4 = f32[2,64,4096]{2,1,0:T(8,128)} fusion(f32[2,64,4096]{2,1,0:T(8,128)} %get-tuple-element.526, f32[2,64,4096]{2,1,0:T(8,128)} %copy-done, f32[2,64,4096]{2,1,0:T(8,128)S(1)} %multiply_add_fusion.8, f32[2]{0:T(128)S(1)} %div.184, f32[2]{0:T(128)S(1)} %div.182, f32[2]{0:T(128)S(1)} %div.180, ...), kind=kLoop, calls=%fused_computation.clone.1 | loop fusion | flops 4718592 | bytes 11534361 | tf_op jit(solution)/shard_map/while/body/eval_jaxpr/sub | solution.py:112
  134.1 5.0 %reshape.180 = f32[2,64,64,64]{3,2,1,0:T(8,128)} reshape(f32[2,64,4096]{2,1,0:T(8,128)} %get-tuple-element.161) | data formatting | bytes 4194304 | tf_op jit(solution)/shard_map/reshape | solution.py:121
  139.1 13.8 %fusion.18 = f32[2,64,64,64]{2,3,1,0:T(8,128)S(1)} fusion(f32[2,64,64,64]{3,2,1,0:T(8,128)} %reshape.180, f32[3,64,64]{2,1,0:T(8,128)S(1)} %copy-done.5), kind=kOutput, calls=%fused_computation.62 | convolution fusion | flops 402653184 | bytes 4227072 | tf_op jit(solution)/shard_map/cz,txyz->txyc/dot_general | solution.py:122
  152.9 5.0 %convolution_bitcast_fusion.2 = f32[2,64,64,64]{2,3,1,0:T(8,128)} fusion(f32[2,64,64,64]{2,3,1,0:T(8,128)S(1)} %fusion.18, f32[3,64,64]{2,1,0:T(8,128)S(1)} %copy-done.5), kind=kOutput, calls=%fused_computation.48 | convolution fusion | flops 402653184 | bytes 6324224 | tf_op jit(solution)/shard_map/by,txyc->txbc/dot_general | solution.py:123
  157.9 5.6 %copy.45 = f32[2,64,64,64]{1,3,2,0:T(8,128)} copy(f32[2,64,64,64]{2,3,1,0:T(8,128)} %convolution_bitcast_fusion.2) | data formatting | bytes 4194304 | tf_op jit(solution)/shard_map/by,txyc->txbc/transpose | solution.py:123
  163.5 6.6 %fusion.12 = f32[2,64,64,64]{3,2,1,0:T(8,128)} fusion(f32[2,64,64,64]{1,3,2,0:T(8,128)} %copy.45, f32[3,64,64]{2,1,0:T(8,128)S(1)} %copy-done.5), kind=kOutput, calls=%fused_computation.56 | convolution fusion | flops 402653184 | bytes 4227072 | tf_op jit(solution)/shard_map/ax,txbc->tabc/dot_general | solution.py:124
  173.9 34.3 %all_to_all.41 = f32[64,2,1,4096]{3,1,2,0:T(2,128)} all-to-all(f32[64,2,1,4096]{3,1,2,0:T(2,128)S(1)} %bitcast.97), channel_id=1, replica_groups=mesh['orb'=64,'trial'=2] {'orb'}, dimensions={0} | all-to-all | bytes 4194304 | tf_op jit(solution)/shard_map/all_to_all | solution.py:35
  210.8 14.3 %all_to_all.42 = f32[64,1,6]{2,1,0:T(1,128)S(1)} all-to-all(f32[64,1,6]{2,1,0:T(1,128)S(1)} %broadcast_in_dim.200), channel_id=1, replica_groups=mesh['orb'=64,'trial'=2] {'orb'}, dimensions={0} | all-to-all | bytes 3072 | tf_op jit(solution)/shard_map/all_to_all | solution.py:12
  228.5 5.0 %all-to-all-start.4 = ((f32[64,2,1,4096]{3,1,2,0:T(2,128)}), f32[64,2,1,4096]{3,1,2,0:T(2,128)S(1)}, u32[]{:S(2)}, u32[]{:S(2)}) async-start(f32[64,2,1,4096]{3,1,2,0:T(2,128)} %broadcast_in_dim.202), calls=%async_computation.4 | async-start | bytes 4194304 | tf_op jit(solution)/shard_map/all_to_all | solution.py:12
  233.4 27.2 %all-to-all-done.4 = f32[64,2,1,4096]{3,1,2,0:T(2,128)S(1)} async-done(((f32[64,2,1,4096]{3,1,2,0:T(2,128)}), f32[64,2,1,4096]{3,1,2,0:T(2,128)S(1)}, u32[]{:S(2)}, u32[]{:S(2)}) %all-to-all-start.4) | async-done | bytes 2097184 | tf_op jit(solution)/shard_map/all_to_all | solution.py:12
  263.2 63.0 %while.27 = (s32[]{:T(128)}, f32[2,64,4096]{2,1,0:T(8,128)}, bf16[2,64,4096]{2,1,0:T(8,128)(2,1)}, f32[2,64,4096]{2,1,0:T(8,128)}, f32[64,4096]{1,0:T(8,128)}, /*index=5*/f32[2]{0:T(128)S(1)}, s32[]{:T(128)}, s32[]{:T(128)}) while((s32[]{:T(128)}, f32[2,64,4096]{2,1,0:T(8,128)}, bf16[2,64,4096]{2,1,0:T(8,128)(2,1)}, ...), condition=%wide.region_22.23_spmd.clone, body=%wide.region_15.22_spmd.clone.sunk | while | flops 34897920 | bytes 182869376 | solution.py:114
  321.2 5.0 %select_subtract_fusion.5 = f32[2,64,4096]{2,1,0:T(8,128)} fusion(f32[2,64,4096]{2,1,0:T(8,128)} %get-tuple-element.550, f32[2,64,4096]{2,1,0:T(8,128)} %copy-done.1, f32[2,64,4096]{2,1,0:T(8,128)S(1)} %multiply_add_fusion.10, f32[2]{0:T(128)S(1)} %div.189, f32[2]{0:T(128)S(1)} %div.187, f32[2]{0:T(128)S(1)} %div.185, ...), kind=kLoop, calls=%fused_computation.23.clone.1 | loop fusion | flops 4718592 | bytes 11534361 | tf_op jit(solution)/shard_map/while/body/eval_jaxpr/sub | solution.py:112
  331.1 13.8 %fusion.16 = f32[2,64,64,64]{2,3,1,0:T(8,128)S(1)} fusion(f32[2,64,64,64]{3,2,1,0:T(8,128)} %reshape.182, f32[3,64,64]{2,1,0:T(8,128)S(1)} %copy-done.6), kind=kOutput, calls=%fused_computation.60 | convolution fusion | flops 402653184 | bytes 4227072 | tf_op jit(solution)/shard_map/cz,txyz->txyc/dot_general | solution.py:122
  344.8 5.0 %convolution_bitcast_fusion.1 = f32[2,64,64,64]{2,3,1,0:T(8,128)} fusion(f32[2,64,64,64]{2,3,1,0:T(8,128)S(1)} %fusion.16, f32[3,64,64]{2,1,0:T(8,128)S(1)} %copy-done.6), kind=kOutput, calls=%fused_computation.47 | convolution fusion | flops 402653184 | bytes 6324224 | tf_op jit(solution)/shard_map/by,txyc->txbc/dot_general | solution.py:123
  349.8 5.6 %copy.50 = f32[2,64,64,64]{1,3,2,0:T(8,128)} copy(f32[2,64,64,64]{2,3,1,0:T(8,128)} %convolution_bitcast_fusion.1) | data formatting | bytes 4194304 | tf_op jit(solution)/shard_map/by,txyc->txbc/transpose | solution.py:123
  355.4 6.6 %fusion.10 = f32[2,64,64,64]{3,2,1,0:T(8,128)} fusion(f32[2,64,64,64]{1,3,2,0:T(8,128)} %copy.50, f32[3,64,64]{2,1,0:T(8,128)S(1)} %copy-done.6), kind=kOutput, calls=%fused_computation.54 | convolution fusion | flops 402653184 | bytes 4227072 | tf_op jit(solution)/shard_map/ax,txbc->tabc/dot_general | solution.py:124
  365.8 34.4 %all_to_all.43 = f32[64,2,1,4096]{3,1,2,0:T(2,128)} all-to-all(f32[64,2,1,4096]{3,1,2,0:T(2,128)S(1)} %bitcast.98), channel_id=1, replica_groups=mesh['orb'=64,'trial'=2] {'orb'}, dimensions={0} | all-to-all | bytes 4194304 | tf_op jit(solution)/shard_map/all_to_all | solution.py:35
  407.8 5.0 %all-to-all-start.7 = ((f32[64,4,4]{2,1,0:T(4,128)}), f32[64,4,4]{2,1,0:T(4,128)S(1)}, u32[]{:S(2)}, u32[]{:S(2)}) async-start(f32[64,4,4]{2,1,0:T(4,128)} %broadcast_in_dim.205), calls=%async_computation.7 | async-start | bytes 262144 | tf_op jit(solution)/shard_map/all_to_all | solution.py:12
  412.9 9.8 %all-to-all-done.7 = f32[64,4,4]{2,1,0:T(4,128)S(1)} async-done(((f32[64,4,4]{2,1,0:T(4,128)}), f32[64,4,4]{2,1,0:T(4,128)S(1)}, u32[]{:S(2)}, u32[]{:S(2)}) %all-to-all-start.7) | async-done | bytes 4128 | tf_op jit(solution)/shard_map/all_to_all | solution.py:12
  (188 shorter events, 156.6 us)
Async XLA Ops:
  0.0 14.3 %copy-start.2 = (f32[2,1,4096]{2,1,0:T(1,128)S(1)}, f32[2,1,4096]{2,1,0:T(1,128)}, u32[]{:S(2)}) copy-start(f32[2,1,4096]{2,1,0:T(1,128)} %param.12) | copy-start | bytes 98308
  2.7 30.1 %all-to-all-start.1 = ((f32[64,1,4096]{2,1,0:T(1,128)}), f32[64,1,4096]{2,1,0:T(1,128)S(1)}, u32[]{:S(2)}, u32[]{:S(2)}) async-start(f32[64,1,4096]{2,1,0:T(1,128)} %broadcast_in_dim.195), calls=%async_computation.1 | async-start | bytes 2097152 | tf_op jit(solution)/shard_map/all_to_all | solution.py:12
  35.2 5.0 %copy-start.13 = (f32[8]{0:T(128)S(1)}, f32[8]{0:T(128)}, u32[]{:S(2)}) copy-start(f32[8]{0:T(128)} %param.17) | copy-start | bytes 100
  35.2 5.0 %copy-start.14 = (s32[2]{0:T(128)S(1)}, s32[2]{0:T(128)}, u32[]{:S(2)}) copy-start(s32[2]{0:T(128)} %param.19) | copy-start | bytes 28
  35.2 5.2 %copy-start.15 = (f32[128]{0:T(128)S(1)}, f32[128]{0:T(128)}, u32[]{:S(2)}) copy-start(f32[128]{0:T(128)} %param.16) | copy-start | bytes 1540
  35.2 5.2 %copy-start.16 = (s32[2]{0:T(128)S(1)}, s32[2]{0:T(128)}, u32[]{:S(2)}) copy-start(s32[2]{0:T(128)} %param.18) | copy-start | bytes 28
  35.2 33.4 %all-to-all-start = ((f32[64,2,1,4096]{3,1,2,0:T(2,128)}), f32[64,2,1,4096]{3,1,2,0:T(2,128)S(1)}, u32[]{:S(2)}, u32[]{:S(2)}) async-start(f32[64,2,1,4096]{3,1,2,0:T(2,128)} %broadcast_in_dim.193), calls=%async_computation | async-start | bytes 4194304 | tf_op jit(solution)/shard_map/all_to_all | solution.py:12
  94.2 1.9 copy-start
  125.3 1.9 copy-start
  134.1 5.0 %copy-start.5 = (f32[3,64,64]{2,1,0:T(8,128)S(1)}, f32[3,64,64]{2,1,0:T(8,128)}, u32[]{:S(2)}) copy-start(f32[3,64,64]{2,1,0:T(8,128)} %param.15) | copy-start | bytes 147460
  208.2 2.2 copy-start.3
  225.3 3.1 copy-start.9
  225.3 3.1 copy-start.11
  225.4 0.6 copy-start.7
  228.5 32.2 %all-to-all-start.4 = ((f32[64,2,1,4096]{3,1,2,0:T(2,128)}), f32[64,2,1,4096]{3,1,2,0:T(2,128)S(1)}, u32[]{:S(2)}, u32[]{:S(2)}) async-start(f32[64,2,1,4096]{3,1,2,0:T(2,128)} %broadcast_in_dim.202), calls=%async_computation.4 | async-start | bytes 4194304 | tf_op jit(solution)/shard_map/all_to_all | solution.py:12
  286.3 1.9 copy-start.1
  317.4 1.9 copy-start.1
  326.3 4.8 %copy-start.6 = (f32[3,64,64]{2,1,0:T(8,128)S(1)}, f32[3,64,64]{2,1,0:T(8,128)}, u32[]{:S(2)}) copy-start(f32[3,64,64]{2,1,0:T(8,128)} %param.15) | copy-start | bytes 147460
  400.2 2.3 copy-start.4
  400.2 2.3 copy-start.8
  400.2 2.3 copy-start.10
  400.2 2.3 copy-start.12
  407.8 14.8 %all-to-all-start.7 = ((f32[64,4,4]{2,1,0:T(4,128)}), f32[64,4,4]{2,1,0:T(4,128)S(1)}, u32[]{:S(2)}, u32[]{:S(2)}) async-start(f32[64,4,4]{2,1,0:T(4,128)} %broadcast_in_dim.205), calls=%async_computation.7 | async-start | bytes 262144 | tf_op jit(solution)/shard_map/all_to_all | solution.py:12
where the time goes:
time: 432 us; the launch traced here: 426 us
  other arithmetic  103 us (24%)
  blocking collectives  86.8 us (20%)
  waiting for transfers between devices  81.8 us (19%)
  local copies, waits for them, and re-layouts  75.2 us (17%)
  matrix products  51.4 us (12%)
  starting transfers between devices  26.5 us (6%)
    all_to_all x4, waiting for transfers between devices, from_everyone(): lax.all_to_all(jnp.broadcast_to(shard[None], (length, *shard.shape)), axi...  81.8 us
    all_to_all x2, blocking collectives, sum_at_owner(): lax.all_to_all(tiles, axis, split_axis=0, concat_axis=0, tiled=True)  68.7 us
    reduce_sum x22, other arithmetic, cell_inner(): return jnp.sum(left_field * right_field, axis=(1, 2))  47.2 us
    dot_general x2, matrix products, coulomb_full(): jnp.einsum('cz,txyz->txyc', factors[2], cube_view, precision=lax.Precisio...  27.5 us
    all_to_all x4, starting transfers between devices, from_everyone(): lax.all_to_all(jnp.broadcast_to(shard[None], (length, *shard.shape)), axi...  26.5 us
    sub x4, other arithmetic, one_orbital(): return (accumulated - density * solved, None)  18.9 us
    all_to_all x2, blocking collectives, from_everyone(): lax.all_to_all(jnp.broadcast_to(shard[None], (length, *shard.shape)), axi...  18.1 us
    slice x12, local copies, waits for them, and re-layouts, neighbour_sum(): grid_field[..., 1:]  14 us
  transfers between devices with their start and end apart: 4, of which 4 were waited for; matrix products, arithmetic and copies ran while one was open for 0% of the time, Pallas kernels for 0%

commit v1 on v0

v1 whole, which is shorter than its diff:
```python
import jax
import jax.numpy as jnp
from jax import lax
from jax.experimental import pallas as pl
from jax.experimental.pallas import tpu as pltpu
from jax.sharding import PartitionSpec as P

G = 64
L = 128
MESH = pl.DeviceIdType.MESH
HIGHEST = lax.Precision.HIGHEST
F32 = jnp.float32
BF16 = jnp.bfloat16
ALL = slice(None)

DIMS = ("x", "z", "y")
STRIDE = {"x": 16, "z": 4, "y": 1}

GROUP = 80
MID = 1.25
EXTRA = 16
SUMS = 8

FIRST_COLORS = (
    (("y", "z", "x"), pl.ds(0, 32)),
    (("z", "x", "y"), pl.ds(32, 24)),
    (("x", "y", "z"), pl.ds(56, 24)),
)
SECOND_COLORS = (
    (("y", "z", "x"), pl.ds(0, 24)),
    (("z", "x", "y"), pl.ds(24, 24)),
    (("x", "y", "z"), pl.ds(48, 24)),
)
SUM_COLORS = (
    (("y", "z", "x"), pl.ds(0, 24)),
    (("z", "x", "y"), pl.ds(24, 24)),
    (("x", "y", "z"), pl.ds(48, 16)),
)


class Place:
    def __init__(self):
        self.orb = lax.axis_index("orb")
        self.trial = lax.axis_index("trial")
        self.at = {
            a: lax.rem(lax.div(self.orb, jnp.int32(STRIDE[a])), jnp.int32(4)) for a in DIMS
        }

    def step(self, axis, by):
        return lax.rem(self.at[axis] + jnp.int32(by % 4), jnp.int32(4))

    def peer(self, axis, by):
        return (self.orb + (self.step(axis, by) - self.at[axis]) * STRIDE[axis], self.trial)

    def partner(self):
        return (self.orb, 1 - self.trial)

    def own(self, ref):
        return ref.at[self.at["x"], self.at["z"], self.at["y"]]

    def region(self, ref, order, phase, index, rows, half=None):
        spec = dict(self.at)
        for a in order[:phase]:
            spec[a] = ALL
        if half is not None:
            spec[order[0]] = pl.ds(2 * half, 2)
        spec[order[phase]] = index
        return ref.at[spec["x"], spec["z"], spec["y"], rows]


def remote(src, dst, send_sem, recv_sem, device):
    copy = pltpu.make_async_remote_copy(
        src_ref=src,
        dst_ref=dst,
        send_sem=send_sem,
        recv_sem=recv_sem,
        device_id=device,
        device_id_type=MESH,
    )
    copy.start()
    return copy


def gather(me, full, colors, send_sem, recv_sem, meanwhile=None):
    sends = []
    for phase in range(3):
        near = []
        for c, (order, rows) in enumerate(colors):
            axis = order[phase]
            mine = me.region(full, order, phase, me.at[axis], rows)
            copies = [
                remote(mine, mine, send_sem.at[c, phase, k], recv_sem.at[c, phase, k], me.peer(axis, by))
                for k, by in enumerate((1, -1, 2) if phase == 0 else (1, -1))
            ]
            near.append(copies)
            sends += copies
        if phase == 0:
            if meanwhile is not None:
                meanwhile()
            for copies in near:
                for copy in copies:
                    copy.wait_recv()
            continue
        far = []
        for c, (order, rows) in enumerate(colors):
            axis = order[phase]
            for half, by in ((0, 1), (1, -1)):
                near[c][half].wait_recv()
                onward = me.region(full, order, phase, me.step(axis, -by), rows, half)
                k = 2 + half
                far.append(
                    remote(onward, onward, send_sem.at[c, phase, k], recv_sem.at[c, phase, k], me.peer(axis, by))
                )
        for copy in far:
            copy.wait_recv()
        sends += far
    return sends


def landing_shapes(colors):
    shapes = []
    for order, rows in colors:
        for phase in (2, 1):
            kept = [a for a in DIMS if a in order[:phase]]
            lead = tuple(2 if a == order[0] else 4 for a in kept)
            shapes.append(pltpu.VMEM((6, *lead, rows.size, L), F32))
        shapes.append(pltpu.VMEM((3, rows.size, L), F32))
    return shapes


def scatter_sums(me, part, landing, colors, send_sem, recv_sem):
    sends = []
    for phase in (2, 1):
        started = []
        for c, (order, rows) in enumerate(colors):
            axis = order[phase]
            land = landing[3 * c + 2 - phase]
            started.append(
                [
                    remote(
                        me.region(part, order, phase, me.step(axis, 2), rows, half),
                        land.at[half],
                        send_sem.at[c, phase, half],
                        recv_sem.at[c, phase, half],
                        me.peer(axis, by),
                    )
                    for half, by in ((0, 1), (1, -1))
                ]
            )
        for c, (order, rows) in enumerate(colors):
            axis = order[phase]
            land = landing[3 * c + 2 - phase]
            for k, half, by in ((2, 1, 1), (3, 0, -1)):
                started[c].append(
                    remote(
                        me.region(part, order, phase, me.step(axis, by), rows, half),
                        land.at[k],
                        send_sem.at[c, phase, k],
                        recv_sem.at[c, phase, k],
                        me.peer(axis, by),
                    )
                )
        for c, (order, rows) in enumerate(colors):
            axis = order[phase]
            land = landing[3 * c + 2 - phase]
            for k, half, by in ((4, 0, 1), (5, 1, -1)):
                started[c][half].wait_recv()
                onward = me.region(part, order, phase, me.step(axis, by), rows, half)
                onward[...] = onward[...] + land[half]
                started[c].append(
                    remote(
                        onward,
                        land.at[k],
                        send_sem.at[c, phase, k],
                        recv_sem.at[c, phase, k],
                        me.peer(axis, by),
                    )
                )
        for c, (order, rows) in enumerate(colors):
            axis = order[phase]
            land = landing[3 * c + 2 - phase]
            for copy in started[c][2:]:
                copy.wait_recv()
            for half, (one, other) in enumerate(((3, 4), (2, 5))):
                mine = me.region(part, order, phase, me.at[axis], rows, half)
                mine[...] = mine[...] + (land[one] + land[other])
            sends += started[c]
    started = []
    for c, (order, rows) in enumerate(colors):
        land = landing[3 * c + 2]
        started.append(
            [
                remote(
                    me.region(part, order, 0, me.step(order[0], by), rows),
                    land.at[by - 1],
                    send_sem.at[c, 0, by],
                    recv_sem.at[c, 0, by],
                    me.peer(order[0], by),
                )
                for by in (1, 2, 3)
            ]
        )
    for c, (order, rows) in enumerate(colors):
        land = landing[3 * c + 2]
        for copy in started[c]:
            copy.wait_recv()
        mine = me.region(part, order, 0, me.at[order[0]], rows)
        mine[...] = mine[...] + ((land[0] + land[1]) + land[2])
        sends += started[c]
    return sends


def lanes():
    return lax.broadcasted_iota(jnp.int32, (1, L), 1)


def swap(values):
    return pltpu.roll(values, G, 1)


def halves(values):
    low = lanes() < G
    first = jnp.sum(jnp.where(low, values, 0.0), axis=1, keepdims=True)
    second = jnp.sum(jnp.where(low, 0.0, values), axis=1, keepdims=True)
    return jnp.where(low, first, second)


def fold(values):
    t = [values[8 * k : 8 * k + 8] for k in range(8)]
    return ((t[0] + t[1]) + (t[2] + t[3])) + ((t[4] + t[5]) + (t[6] + t[7]))


def column(values):
    return jnp.sum(values, axis=0, keepdims=True)


def step_weights(m, shift):
    a = [m[k + 1] + shift * m[k] for k in range(5)]
    low10 = a[1] / a[0]
    low20 = a[2] / a[0]
    pivot1 = a[2] - low10 * a[1]
    some = pivot1 > 1e-6 * a[2]
    cross = a[3] - low10 * a[2]
    low21 = jnp.where(some, cross / pivot1, 0.0)
    pivot2 = a[4] - low20 * a[2] - low21 * cross
    more = some & (pivot2 > 1e-6 * a[4])
    y1 = m[1] - low10 * m[0]
    y2 = m[2] - low20 * m[0] - low21 * y1
    c2 = jnp.where(more, y2 / pivot2, 0.0)
    c1 = jnp.where(some, y1 / pivot1, 0.0) - low21 * c2
    c0 = m[0] / a[0] - low10 * c1 - low20 * c2
    return 2.0 * c0, 2.0 * c1, 2.0 * c2


def respond(fields, dens, pot, shifts, kx, part, trial_lines):
    u0, u1, u2 = fields
    slots = range(dens.shape[0])
    low = lanes() % G == 0
    high = lanes() % G == G - 1

    def begin(y, _):
        v = trial_lines(y)
        for s in slots:
            u0[s, y + 1, 8:72] = v * dens[s, y]
        return 0

    lax.fori_loop(0, G, begin, 0)

    def centred(u, s, y, diagonal):
        c = u[s, y + 1, 8:72]
        along_z = jnp.where(high, 0.0, pltpu.roll(c, L - 1, 1)) + jnp.where(low, 0.0, pltpu.roll(c, 1, 1))
        along_y = u[s, y, 8:72] + u[s, y + 2, 8:72]
        along_x = u[s, y + 1, 7:71] + u[s, y + 1, 9:73]
        return c, diagonal * c - (along_z + along_y + along_x)

    zero = jnp.zeros((8, L), F32)

    def first_power(y, sums):
        diagonal = pot[y]
        out = []
        for s in slots:
            c, q = centred(u0, s, y, diagonal)
            u1[s, y + 1, 8:72] = q
            a = sums[s]
            out.append((a[0] + fold(c * c), a[1] + fold(c * q), a[2] + fold(q * q)))
        return tuple(out)

    low_sums = lax.fori_loop(0, G, first_power, tuple((zero,) * 3 for _ in slots))

    def second_power(y, sums):
        diagonal = pot[y]
        out = []
        for s in slots:
            c, q = centred(u1, s, y, diagonal)
            u2[s, y + 1, 8:72] = q
            a = sums[s]
            out.append((a[0] + fold(c * q), a[1] + fold(q * q)))
        return tuple(out)

    high_sums = lax.fori_loop(0, G, second_power, tuple((zero,) * 2 for _ in slots))

    def third_power(y, sums):
        diagonal = pot[y]
        out = []
        for s in slots:
            c = u2[s, y + 1, 8:72]
            ahead = jnp.where(high, 0.0, pltpu.roll(c, L - 1, 1)) + u2[s, y + 2, 8:72] + u2[s, y + 1, 9:73]
            out.append(sums[s] + fold(c * (diagonal * c - (ahead + ahead))))
        return tuple(out)

    top_sums = lax.fori_loop(0, G, third_power, tuple(zero for _ in slots))

    weights = []
    for s in slots:
        moments = [halves(column(t)) for t in (*low_sums[s], *high_sums[s], top_sums[s])]
        weights.append(step_weights(moments, shifts[s]))

    rows = part.reshape(G * G, L)

    def finish(y, _):
        total = None
        for s in slots:
            w = [c * u[s, y + 1, 8:72] for c, u in zip(weights[s], (u0, u1, u2))]
            term = (w[0] + w[1] + w[2]) * dens[s, y]
            total = term if total is None else total + term
        total = -total
        upper = total.astype(BF16)
        lower = (total - upper.astype(F32)).astype(BF16)
        stacked = jnp.concatenate([upper, upper, lower], axis=0)
        rows[pl.ds(y, G, stride=G), :] = jnp.dot(kx, stacked, preferred_element_type=F32)
        return 0

    lax.fori_loop(0, G, finish, 0)


def kernel(
    energies,
    frequencies,
    orbital_ids,
    freq_index,
    trials,
    orbitals,
    potential,
    coulomb,
    out,
    full,
    mapped,
    pot_other,
    dens,
    pot,
    u0,
    u1,
    u2,
    part,
    other,
    small,
    first_send,
    first_recv,
    second_send,
    second_recv,
    sum_send,
    sum_recv,
    pair_send,
    pair_recv,
    small_send,
    small_recv,
    *landing,
):
    me = Place()
    slots = range(dens.shape[0])
    half = lanes() < G

    barrier = pltpu.get_barrier_semaphore()
    peers = [me.peer(a, by) for a in DIMS for by in (1, 2, 3)] + [me.partner()]
    for peer in peers:
        pl.semaphore_signal(barrier, inc=1, device_id=peer, device_id_type=MESH)

    plane = me.own(full)
    for k in range(G // 2):
        a = trials[0, :, k * L : (k + 1) * L]
        b = trials[1, :, k * L : (k + 1) * L]
        plane[2 * k : 2 * k + 1, :] = jnp.where(half, a, swap(b))
        plane[2 * k + 1 : 2 * k + 2, :] = jnp.where(half, swap(a), b)
    for k in range(EXTRA):
        start = pl.multiple_of((me.trial * EXTRA + k) * L, L)
        plane[G + k : G + k + 1, :] = potential[:, pl.ds(start, L)]

    pl.semaphore_wait(barrier, len(peers))

    def prepare():
        def clear(y, _):
            for u in (u0, u1, u2):
                for s in slots:
                    u[s, y, 0:8] = jnp.zeros((8, L), F32)
                    u[s, y, 72:80] = jnp.zeros((8, L), F32)
            return 0

        for u in (u0, u1, u2):
            for s in slots:
                u[s, 0] = jnp.zeros((GROUP, L), F32)
                u[s, G + 1] = jnp.zeros((GROUP, L), F32)
        lax.fori_loop(1, G + 1, clear, 0)

        def spread_out(k, _):
            for s in slots:
                t = orbitals[s, :, pl.ds(pl.multiple_of(k * L, L), L)].astype(F32)
                turned = swap(t)
                dens[s, 2 * k] = jnp.where(half, t, turned)
                dens[s, 2 * k + 1] = jnp.where(half, turned, t)
            return 0

        lax.fori_loop(0, G // 2, spread_out, 0)

    sends = gather(me, full, FIRST_COLORS, first_send, first_recv, prepare)

    pot_lines = full.at[:, :, :, pl.ds(G, EXTRA)]
    pot_copy = remote(pot_lines, pot_other, pair_send.at[0], pair_recv.at[0], me.partner())

    full_rows = full.reshape(G * (G + EXTRA), L)
    other_rows = pot_other.reshape(G * EXTRA, L)
    mapped_rows = mapped.reshape(G * (G + SUMS), L)

    def level(j, base, t):
        turned = swap(t)
        y = 2 * (base + j)
        pot[y] = 2.0 * jnp.where(half, t, turned) - 2.0 * MID
        pot[y + 1] = 2.0 * jnp.where(half, turned, t) - 2.0 * MID

    def own_level(j, _):
        level(j, me.trial * EXTRA, full_rows[pl.ds(G + j, G, stride=G + EXTRA), :])
        return 0

    def other_level(j, _):
        level(j, (1 - me.trial) * EXTRA, other_rows[pl.ds(j, G, stride=EXTRA), :])
        return 0

    lax.fori_loop(0, EXTRA, own_level, 0)
    pot_copy.wait_recv()
    lax.fori_loop(0, EXTRA, other_level, 0)

    shifts = []
    for s in slots:
        level_shift = frequencies[freq_index[s]] - energies[orbital_ids[s]]
        shifts.append(2.0 * (3.0 + level_shift) + 2.0 * MID)

    kx = coulomb[0]
    kx_upper = kx.astype(BF16)
    kx_lower = (kx - kx_upper.astype(F32)).astype(BF16)
    kx_parts = jnp.concatenate([kx_upper, kx_lower, kx_upper], axis=1)
    kz = jnp.concatenate([coulomb[2], coulomb[2]], axis=1)
    kz = jnp.concatenate([kz, kz], axis=0)
    same = (lax.broadcasted_iota(jnp.int32, (L, L), 0) < G) == (lax.broadcasted_iota(jnp.int32, (L, L), 1) < G)
    kz = jnp.where(same, kz, 0.0)

    def in_plane(values):
        turned = lax.dot_general(
            values, kz, (((1,), (1,)), ((), ())), precision=HIGHEST, preferred_element_type=F32
        )
        return jnp.dot(coulomb[1], turned, precision=HIGHEST, preferred_element_type=F32)

    fields = (u0, u1, u2)
    total = me.own(part)
    respond(
        fields, dens, pot, shifts, kx_parts, part, lambda y: full_rows[pl.ds(y, G, stride=G + EXTRA), :]
    )
    n = len(landing) // 2
    part_sends = scatter_sums(me, part, landing[:n], SUM_COLORS, sum_send.at[0], sum_recv.at[0])
    own_mapped = in_plane(total[...])
    own_trials = plane[0:G, :]
    sums = me.own(mapped)
    sums[0:G, :] = own_mapped
    sums[G : G + 1, :] = column(fold(own_trials * own_trials))
    sums[G + 1 : G + 2, :] = column(fold(own_trials * own_mapped))
    sums[G + 2 : G + 3, :] = column(fold(own_mapped * own_mapped))
    sums[G + 3 : G + SUMS, :] = jnp.zeros((SUMS - 3, L), F32)
    sends += gather(me, mapped, SECOND_COLORS, second_send, second_recv)

    all_sums = jnp.zeros((SUMS, L), F32)
    for x in range(4):
        for z in range(4):
            for y in range(4):
                all_sums = all_sums + mapped[x, z, y, G : G + SUMS, :]
    squares = halves(all_sums[0:1])
    center = halves(all_sums[1:2]) / squares
    spread = jnp.sqrt(halves(all_sums[2:3]) / squares)
    unspread = 1.0 / spread

    def first_lines(y):
        t = full_rows[pl.ds(y, G, stride=G + EXTRA), :]
        m = mapped_rows[pl.ds(y, G, stride=G + SUMS), :]
        return (m - center * t) * unspread

    for copy in part_sends:
        copy.wait_send()
    respond(fields, dens, pot, shifts, kx_parts, part, first_lines)
    part_sends = scatter_sums(me, part, landing[n:], SUM_COLORS, sum_send.at[1], sum_recv.at[1])
    own_first = (own_mapped - center * own_trials) * unspread
    second = 2.0 * (in_plane(total[...]) - center * own_first) * unspread - own_trials

    other[0] = second
    swap_copy = remote(other.at[0], other.at[1], pair_send.at[1], pair_recv.at[1], me.partner())
    swap_copy.wait_recv()
    theirs = other[1]
    is_first = me.trial == 0
    a = jnp.where(is_first, second, theirs)
    b = jnp.where(is_first, theirs, second)
    turned_a = swap(a)
    turned_b = swap(b)
    for k, product in enumerate((a * a, a * turned_a, b * b, b * turned_b, a * b, a * turned_b)):
        small[0, 0, k : k + 1] = column(fold(product))
    small[0, 0, 6:8] = jnp.zeros((2, L), F32)
    sends += part_sends + [pot_copy, swap_copy]
    for phase, axis in enumerate(DIMS):
        copies = [
            remote(
                small.at[phase, 0],
                small.at[phase, by],
                small_send.at[phase, by],
                small_recv.at[phase, by],
                me.peer(axis, by),
            )
            for by in (1, 2, 3)
        ]
        for copy in copies:
            copy.wait_recv()
        small[phase + 1, 0] = (small[phase, 0] + small[phase, 1]) + (small[phase, 2] + small[phase, 3])
        sends += copies
    block = small[3, 0] * (1.0 / float(G**3))

    def entry(row, upper):
        picked = jnp.where(half, 0.0, block[row : row + 1]) if upper else jnp.where(half, block[row : row + 1], 0.0)
        return jnp.sum(picked, axis=1, keepdims=True)

    gram = {
        (0, 0): entry(0, False),
        (1, 1): entry(0, True),
        (1, 0): entry(1, False),
        (2, 2): entry(2, False),
        (3, 3): entry(2, True),
        (3, 2): entry(3, False),
        (2, 0): entry(4, False),
        (3, 1): entry(4, True),
        (3, 0): entry(5, False),
        (2, 1): entry(5, True),
    }
    lower = {}
    for j in range(4):
        rest = gram[j, j]
        for k in range(j):
            rest = rest - lower[j, k] * lower[j, k]
        lower[j, j] = jnp.sqrt(rest)
        for i in range(j + 1, 4):
            rest = gram[i, j]
            for k in range(j):
                rest = rest - lower[i, k] * lower[j, k]
            lower[i, j] = rest / lower[j, j]
    nothing = jnp.zeros((1, 1), F32)
    inverse = {(i, j): nothing for i in range(4) for j in range(4)}
    for j in range(4):
        inverse[j, j] = 1.0 / lower[j, j]
        for i in range(j + 1, 4):
            rest = nothing
            for k in range(j, i):
                rest = rest - lower[i, k] * inverse[k, j]
            inverse[i, j] = rest / lower[i, i]
    copies = (
        jnp.where(half, a, turned_a),
        jnp.where(half, turned_a, a),
        jnp.where(half, b, turned_b),
        jnp.where(half, turned_b, b),
    )
    result = None
    for u in range(4):
        here = jnp.where(is_first, inverse[0, u], inverse[2, u])
        there = jnp.where(is_first, inverse[1, u], inverse[3, u])
        term = jnp.where(half, here, there) * copies[u]
        result = term if result is None else result + term
    other[2] = result
    for k in range(G // 2):
        a = other[2, 2 * k : 2 * k + 1, :]
        b = other[2, 2 * k + 1 : 2 * k + 2, :]
        out[0, :, k * L : (k + 1) * L] = jnp.where(half, a, swap(b))
        out[1, :, k * L : (k + 1) * L] = jnp.where(half, swap(a), b)
    for copy in sends:
        copy.wait_send()


def shards(trials, orbitals, potential, coulomb, energies, frequencies, orbital_ids, freq_index):
    slots = orbitals.shape[0]
    vmem = pl.BlockSpec(memory_space=pltpu.VMEM)
    smem = pl.BlockSpec(memory_space=pltpu.SMEM)
    dma = pltpu.SemaphoreType.DMA
    field = pltpu.VMEM((slots, G + 2, GROUP, L), F32)
    return pl.pallas_call(
        kernel,
        out_shape=jax.ShapeDtypeStruct(trials.shape, F32),
        in_specs=[smem] * 4 + [vmem] * 4,
        out_specs=vmem,
        scratch_shapes=[
            pltpu.VMEM((4, 4, 4, G + EXTRA, L), F32),
            pltpu.VMEM((4, 4, 4, G + SUMS, L), F32),
            pltpu.VMEM((4, 4, 4, EXTRA, L), F32),
            pltpu.VMEM((slots, G, G, L), F32),
            pltpu.VMEM((G, G, L), F32),
            field,
            field,
            field,
            pltpu.VMEM((4, 4, 4, G, L), F32),
            pltpu.VMEM((3, G, L), F32),
            pltpu.VMEM((4, 4, 8, L), F32),
            dma((3, 3, 4)),
            dma((3, 3, 4)),
            dma((3, 3, 4)),
            dma((3, 3, 4)),
            dma((2, 3, 3, 6)),
            dma((2, 3, 3, 6)),
            dma((2,)),
            dma((2,)),
            dma((3, 4)),
            dma((3, 4)),
            *landing_shapes(SUM_COLORS),
            *landing_shapes(SUM_COLORS),
        ],
        compiler_params=pltpu.CompilerParams(
            collective_id=0, has_side_effects=True, vmem_limit_bytes=60 * 2**20
        ),
        name="filter",
    )(energies, frequencies, orbital_ids, freq_index, trials, orbitals, potential, coulomb)


def solution(mesh):
    in_specs = (
        P("trial", "orb", None),
        P("orb", None, None),
        P("orb", None),
        P(),
        P(),
        P(),
        P("orb"),
        P("orb"),
    )
    return jax.shard_map(
        shards, mesh=mesh, in_specs=in_specs, out_specs=P("trial", "orb", None), check_vma=False
    )
```

time: 432 us -> 181 us (0.42); the launches traced: 426 us -> 181 us
  Pallas kernels: 0 us -> 180 us
  other arithmetic: 103 us -> 0 us
  blocking collectives: 86.8 us -> 0 us
  waiting for transfers between devices: 81.8 us -> 0 us
  local copies, waits for them, and re-layouts: 75.2 us -> 1.38 us
  matrix products: 51.4 us -> 0 us
  starting transfers between devices: 26.5 us -> 0 us
    pallas_call x0 -> x1, Pallas kernels: none -> 180 us  [shards(): pl.pallas_call(kernel, out_shape=jax.ShapeDtypeStruct(trials.shape, F32),...]
    all_to_all x4 -> x0, blocking collectives: 86.8 us -> none  [the longest x2 68.7 us: sum_at_owner(): lax.all_to_all(tiles, axis, split_axis=0, concat_axis=0, tiled=True)]
    all_to_all x4 -> x0, waiting for transfers between devices: 81.8 us -> none  [from_everyone(): lax.all_to_all(jnp.broadcast_to(shard[None], (length, *shard.shape)), axi...]
    reduce_sum x28 -> x0, other arithmetic: 52.2 us -> none  [the longest x22 47.2 us: cell_inner(): return jnp.sum(left_field * right_field, axis=(1, 2))]
    dot_general x8 -> x0, matrix products: 51.2 us -> none  [the longest x2 27.5 us: coulomb_full(): jnp.einsum('cz,txyz->txyc', factors[2], cube_view, precision=lax.Precisio...]
    slice x36 -> x0, local copies, waits for them, and re-layouts: 27.6 us -> none  [the longest x12 14 us: neighbour_sum(): grid_field[..., 1:]]
    all_to_all x4 -> x0, starting transfers between devices: 26.5 us -> none  [from_everyone(): lax.all_to_all(jnp.broadcast_to(shard[None], (length, *shard.shape)), axi...]
    sub x6 -> x0, other arithmetic: 19 us -> none  [the longest x4 18.9 us: one_orbital(): return (accumulated - density * solved, None)]
  transfers between devices with their start and end apart: 4 -> 0, of which waited for: 4 -> 0; matrix products, arithmetic and copies ran while one was open for 0% -> 0% of each run, Pallas kernels for 0% -> 0%
where the time goes in v1:
time: 181 us
  Pallas kernels  180 us (99%)
    pallas_call x1, Pallas kernels, shards(): pl.pallas_call(kernel, out_shape=jax.ShapeDtypeStruct(trials.shape, F32),...  180 us

profile of v1, /device:TPU:0, one launch (start us, length us, event | category | flops | bytes accessed | tf_op | source)
XLA Modules:
  0.0 181.1 jit_solution(2693375741947019312)
XLA Ops:
  0.0 179.7 %filter.1 = f32[2,1,4096]{2,1,0:T(1,128)} custom-call(f32[128]{0:T(128)} %energies.1, f32[8]{0:T(128)} %frequencies.1, s32[2]{0:T(128)} %orbital_ids.1, s32[2]{0:T(128)} %freq_index.1, f32[2,1,4096]{2,1,0:T(1,128)} %trials.1, bf16[2,64,4096]{2,1,0:T(8,128)(2,1)} %orbitals.1, f32[1,4096]{1,0:T(1,128)} %potential.1, f32[3,64,64]{2,1,0:T(8,128)} %coulomb.1), custom_call_target="tpu_custom_call" | custom-call | tf_op jit(solution)/shard_map/filter/pallas_call | solution.py:594
  179.7 1.4 copy.10

commit v2 on v1

--- a/solution.py
+++ b/solution.py
@@ -17,6 +17,7 @@
 STRIDE = {"x": 16, "z": 4, "y": 1}
 
 GROUP = 80
+LINES = 8
 MID = 1.25
 EXTRA = 16
 SUMS = 8
@@ -83,38 +84,81 @@
 
 def gather(me, full, colors, send_sem, recv_sem, meanwhile=None):
     sends = []
-    for phase in range(3):
-        near = []
-        for c, (order, rows) in enumerate(colors):
-            axis = order[phase]
-            mine = me.region(full, order, phase, me.at[axis], rows)
-            copies = [
-                remote(mine, mine, send_sem.at[c, phase, k], recv_sem.at[c, phase, k], me.peer(axis, by))
-                for k, by in enumerate((1, -1, 2) if phase == 0 else (1, -1))
-            ]
-            near.append(copies)
-            sends += copies
-        if phase == 0:
-            if meanwhile is not None:
-                meanwhile()
-            for copies in near:
-                for copy in copies:
-                    copy.wait_recv()
-            continue
-        far = []
-        for c, (order, rows) in enumerate(colors):
-            axis = order[phase]
-            for half, by in ((0, 1), (1, -1)):
-                near[c][half].wait_recv()
-                onward = me.region(full, order, phase, me.step(axis, -by), rows, half)
-                k = 2 + half
-                far.append(
-                    remote(onward, onward, send_sem.at[c, phase, k], recv_sem.at[c, phase, k], me.peer(axis, by))
-                )
-        for copy in far:
-            copy.wait_recv()
-        sends += far
+    state = []
+    for i, (order, rows) in enumerate(colors):
+        state.append(Route(me, full, order, rows, send_sem.at[i], recv_sem.at[i], sends))
+    for r in state:
+        r.first = [r.send(r.planes(), k, 0, by) for k, by in enumerate((1, -1, 2))]
+    for r in state:
+        wait_all(r.first)
+        r.second = [r.send(r.planes(a=ALL), 3 + k, 1, by) for k, by in enumerate((1, -1))]
+        r.third = {0: r.outward(0)}
+    if meanwhile is not None:
+        meanwhile()
+    for r in state:
+        r.second_far = []
+        for half, by in ((0, 1), (1, -1)):
+            r.second[half].wait_recv()
+            r.second_far.append(r.send(r.planes(a=half, b=-by), 5 + half, 1, by))
+            r.third[-by] = r.outward(-by)
+    for r in state:
+        r.pass_on(0)
+    for r in state:
+        wait_all(r.second_far)
+        r.third[2] = r.outward(2)
+    for group in (-1, 1, 2):
+        for r in state:
+            r.pass_on(group)
+    for r in state:
+        wait_all(r.last)
     return sends
+
+
+def wait_all(copies):
+    for copy in copies:
+        copy.wait_recv()
+
+
+class Route:
+    def __init__(self, me, ref, order, rows, send_sem, recv_sem, sends):
+        self.me, self.ref, self.order, self.rows = me, ref, order, rows
+        self.send_sem, self.recv_sem, self.sends = send_sem, recv_sem, sends
+        self.last = []
+
+    def planes(self, a=None, b=0, c=0):
+        me, (da, db, dc) = self.me, self.order
+        spec = {db: me.step(db, b), dc: me.step(dc, c)}
+        if a is None:
+            spec[da] = me.at[da]
+        elif a is ALL:
+            spec[da] = ALL
+        else:
+            spec[da] = pl.ds(2 * a, 2)
+        return self.ref.at[spec["x"], spec["z"], spec["y"], self.rows]
+
+    def send(self, src, k, axis, by, dst=None):
+        copy = remote(
+            src,
+            src if dst is None else dst,
+            self.send_sem.at[k],
+            self.recv_sem.at[k],
+            self.me.peer(self.order[axis], by),
+        )
+        self.sends.append(copy)
+        return copy
+
+    def slot(self, group):
+        return 7 + 4 * (group % 4)
+
+    def outward(self, group):
+        k = self.slot(group)
+        return [self.send(self.planes(a=ALL, b=group), k + n, 2, by) for n, by in enumerate((1, -1))]
+
+    def pass_on(self, group):
+        k = self.slot(group) + 2
+        for half, by in ((0, 1), (1, -1)):
+            self.third[group][half].wait_recv()
+            self.last.append(self.send(self.planes(a=half, b=group, c=-by), k + half, 2, by))
 
 
 def landing_shapes(colors):
@@ -252,11 +296,20 @@
     return 2.0 * c0, 2.0 * c1, 2.0 * c2
 
 
+def split(values):
+    upper = values.astype(BF16)
+    return upper, (values - upper.astype(F32)).astype(BF16)
+
+
 def respond(fields, dens, pot, shifts, kx, part, trial_lines):
-    u0, u1, u2 = fields
+    u0, u1, u2, near_even, near_odd, stack_even, stack_odd = fields
     slots = range(dens.shape[0])
-    low = lanes() % G == 0
-    high = lanes() % G == G - 1
+    lines = near_even.shape[1]
+    chunks = G // lines
+    row = lax.broadcasted_iota(jnp.int32, (2 * L, L), 0) % L
+    col = lax.broadcasted_iota(jnp.int32, (2 * L, L), 1)
+    beside = (jnp.abs(row - col) == 1) & ((row < G) == (col < G))
+    beside = jnp.where(beside, 1.0, 0.0).astype(BF16)
 
     def begin(y, _):
         v = trial_lines(y)
@@ -264,51 +317,58 @@
             u0[s, y + 1, 8:72] = v * dens[s, y]
         return 0
 
-    lax.fori_loop(0, G, begin, 0)
-
-    def centred(u, s, y, diagonal):
+    lax.fori_loop(0, G, begin, 0, unroll=4)
+
+    def along_z(u, chunk, near):
+        for k in range(lines):
+            y = chunk * lines + k
+            upper, lower = split(jnp.concatenate([u[s, y + 1, 8:72] for s in slots], axis=0))
+            sums = jnp.dot(jnp.concatenate([upper, lower], axis=1), beside, preferred_element_type=F32)
+            for s in slots:
+                near[s, k] = sums[G * s : G * s + G]
+
+    def sweep(u, at_line, sums):
+        along_z(u, 0, near_even)
+
+        def pair(j, sums):
+            for near, ahead, chunk in ((near_even, near_odd, 2 * j), (near_odd, near_even, 2 * j + 1)):
+                along_z(u, lax.rem(chunk + 1, jnp.int32(chunks)), ahead)
+                for k in range(lines):
+                    y = chunk * lines + k
+                    diagonal = pot[y]
+                    sums = tuple(at_line(s, y, diagonal, near[s, k], sums[s]) for s in slots)
+            return sums
+
+        return lax.fori_loop(0, chunks // 2, pair, sums)
+
+    def centred(u, s, y, diagonal, near):
         c = u[s, y + 1, 8:72]
-        along_z = jnp.where(high, 0.0, pltpu.roll(c, L - 1, 1)) + jnp.where(low, 0.0, pltpu.roll(c, 1, 1))
         along_y = u[s, y, 8:72] + u[s, y + 2, 8:72]
         along_x = u[s, y + 1, 7:71] + u[s, y + 1, 9:73]
-        return c, diagonal * c - (along_z + along_y + along_x)
+        return c, diagonal * c - (near + (along_y + along_x))
 
     zero = jnp.zeros((8, L), F32)
 
-    def first_power(y, sums):
-        diagonal = pot[y]
-        out = []
-        for s in slots:
-            c, q = centred(u0, s, y, diagonal)
-            u1[s, y + 1, 8:72] = q
-            a = sums[s]
-            out.append((a[0] + fold(c * c), a[1] + fold(c * q), a[2] + fold(q * q)))
-        return tuple(out)
-
-    low_sums = lax.fori_loop(0, G, first_power, tuple((zero,) * 3 for _ in slots))
-
-    def second_power(y, sums):
-        diagonal = pot[y]
-        out = []
-        for s in slots:
-            c, q = centred(u1, s, y, diagonal)
-            u2[s, y + 1, 8:72] = q
-            a = sums[s]
-            out.append((a[0] + fold(c * q), a[1] + fold(q * q)))
-        return tuple(out)
-
-    high_sums = lax.fori_loop(0, G, second_power, tuple((zero,) * 2 for _ in slots))
-
-    def third_power(y, sums):
-        diagonal = pot[y]
-        out = []
-        for s in slots:
-            c = u2[s, y + 1, 8:72]
-            ahead = jnp.where(high, 0.0, pltpu.roll(c, L - 1, 1)) + u2[s, y + 2, 8:72] + u2[s, y + 1, 9:73]
-            out.append(sums[s] + fold(c * (diagonal * c - (ahead + ahead))))
-        return tuple(out)
-
-    top_sums = lax.fori_loop(0, G, third_power, tuple(zero for _ in slots))
+    def first_power(s, y, diagonal, near, a):
+        c, q = centred(u0, s, y, diagonal, near)
+        u1[s, y + 1, 8:72] = q
+        return a[0] + fold(c * c), a[1] + fold(c * q), a[2] + fold(q * q)
+
+    low_sums = sweep(u0, first_power, tuple((zero,) * 3 for _ in slots))
+
+    def second_power(s, y, diagonal, near, a):
+        c, q = centred(u1, s, y, diagonal, near)
+        u2[s, y + 1, 8:72] = q
+        return a[0] + fold(c * q), a[1] + fold(q * q)
+
+    high_sums = sweep(u1, second_power, tuple((zero,) * 2 for _ in slots))
+
+    def third_power(s, y, diagonal, near, a):
+        c = u2[s, y + 1, 8:72]
+        ahead = u2[s, y + 2, 8:72] + u2[s, y + 1, 9:73]
+        return a + fold(c * (diagonal * c - (near + (ahead + ahead))))
+
+    top_sums = sweep(u2, third_power, tuple(zero for _ in slots))
 
     weights = []
     for s in slots:
@@ -317,20 +377,33 @@
 
     rows = part.reshape(G * G, L)
 
-    def finish(y, _):
-        total = None
-        for s in slots:
-            w = [c * u[s, y + 1, 8:72] for c, u in zip(weights[s], (u0, u1, u2))]
-            term = (w[0] + w[1] + w[2]) * dens[s, y]
-            total = term if total is None else total + term
-        total = -total
-        upper = total.astype(BF16)
-        lower = (total - upper.astype(F32)).astype(BF16)
-        stacked = jnp.concatenate([upper, upper, lower], axis=0)
-        rows[pl.ds(y, G, stride=G), :] = jnp.dot(kx, stacked, preferred_element_type=F32)
+    def gathered(j, stack):
+        for k in range(2):
+            y = 2 * j + k
+            total = None
+            for s in slots:
+                w = [c * u[s, y + 1, 8:72] for c, u in zip(weights[s], (u0, u1, u2))]
+                term = (w[0] + w[1] + w[2]) * dens[s, y]
+                total = term if total is None else total + term
+            upper, lower = split(-total)
+            stack[0:G, k * L : k * L + L] = upper
+            stack[G : 2 * G, k * L : k * L + L] = upper
+            stack[2 * G : 3 * G, k * L : k * L + L] = lower
+
+    def mixed(j, stack):
+        sums = jnp.dot(kx, stack[...], preferred_element_type=F32)
+        for k in range(2):
+            rows[pl.ds(2 * j + k, G, stride=G), :] = sums[:, k * L : k * L + L]
+
+    gathered(0, stack_even)
+
+    def finish(j, _):
+        for stack, ahead, y_pair in ((stack_even, stack_odd, 2 * j), (stack_odd, stack_even, 2 * j + 1)):
+            gathered(lax.rem(y_pair + 1, jnp.int32(G // 2)), ahead)
+            mixed(y_pair, stack)
         return 0
 
-    lax.fori_loop(0, G, finish, 0)
+    lax.fori_loop(0, G // 4, finish, 0)
 
 
 def kernel(
@@ -351,6 +424,10 @@
     u0,
     u1,
     u2,
+    near_even,
+    near_odd,
+    stack_even,
+    stack_odd,
     part,
     other,
     small,
@@ -458,7 +535,7 @@
         )
         return jnp.dot(coulomb[1], turned, precision=HIGHEST, preferred_element_type=F32)
 
-    fields = (u0, u1, u2)
+    fields = (u0, u1, u2, near_even, near_odd, stack_even, stack_odd)
     total = me.own(part)
     respond(
         fields, dens, pot, shifts, kx_parts, part, lambda y: full_rows[pl.ds(y, G, stride=G + EXTRA), :]
@@ -591,6 +668,8 @@
     smem = pl.BlockSpec(memory_space=pltpu.SMEM)
     dma = pltpu.SemaphoreType.DMA
     field = pltpu.VMEM((slots, G + 2, GROUP, L), F32)
+    near = pltpu.VMEM((slots, LINES, G, L), F32)
+    stack = pltpu.VMEM((3 * G, 2 * L), BF16)
     return pl.pallas_call(
         kernel,
         out_shape=jax.ShapeDtypeStruct(trials.shape, F32),
@@ -605,13 +684,17 @@
             field,
             field,
             field,
+            near,
+            near,
+            stack,
+            stack,
             pltpu.VMEM((4, 4, 4, G, L), F32),
             pltpu.VMEM((3, G, L), F32),
             pltpu.VMEM((4, 4, 8, L), F32),
-            dma((3, 3, 4)),
-            dma((3, 3, 4)),
-            dma((3, 3, 4)),
-            dma((3, 3, 4)),
+            dma((3, 23)),
+            dma((3, 23)),
+            dma((3, 23)),
+            dma((3, 23)),
             dma((2, 3, 3, 6)),
             dma((2, 3, 3, 6)),
             dma((2,)),

time: 181 us -> 140 us (0.77)
  Pallas kernels: 180 us -> 138 us
    pallas_call x1, Pallas kernels: 180 us -> 138 us  [shards(): pl.pallas_call(kernel, out_shape=jax.ShapeDtypeStruct(trials.shape, F32),...]
where the time goes in v2:
time: 140 us
  Pallas kernels  138 us (99%)
    pallas_call x1, Pallas kernels, shards(): pl.pallas_call(kernel, out_shape=jax.ShapeDtypeStruct(trials.shape, F32),...  138 us

profile of v2, /device:TPU:0, one launch (start us, length us, event | category | flops | bytes accessed | tf_op | source)
XLA Modules:
  0.0 139.7 jit_solution(13803547674039484883)
XLA Ops:
  0.0 138.4 %filter.1 = f32[2,1,4096]{2,1,0:T(1,128)} custom-call(f32[128]{0:T(128)} %energies.1, f32[8]{0:T(128)} %frequencies.1, s32[2]{0:T(128)} %orbital_ids.1, s32[2]{0:T(128)} %freq_index.1, f32[2,1,4096]{2,1,0:T(1,128)} %trials.1, bf16[2,64,4096]{2,1,0:T(8,128)(2,1)} %orbitals.1, f32[1,4096]{1,0:T(1,128)} %potential.1, f32[3,64,64]{2,1,0:T(8,128)} %coulomb.1), custom_call_target="tpu_custom_call" | custom-call | tf_op jit(solution)/shard_map/filter/pallas_call | solution.py:673
  138.4 1.4 copy.10

commit v3 on v2

--- a/solution.py
+++ b/solution.py
@@ -59,15 +59,6 @@
     def own(self, ref):
         return ref.at[self.at["x"], self.at["z"], self.at["y"]]
 
-    def region(self, ref, order, phase, index, rows, half=None):
-        spec = dict(self.at)
-        for a in order[:phase]:
-            spec[a] = ALL
-        if half is not None:
-            spec[order[0]] = pl.ds(2 * half, 2)
-        spec[order[phase]] = index
-        return ref.at[spec["x"], spec["z"], spec["y"], rows]
-
 
 def remote(src, dst, send_sem, recv_sem, device):
     copy = pltpu.make_async_remote_copy(
@@ -84,34 +75,37 @@
 
 def gather(me, full, colors, send_sem, recv_sem, meanwhile=None):
     sends = []
-    state = []
-    for i, (order, rows) in enumerate(colors):
-        state.append(Route(me, full, order, rows, send_sem.at[i], recv_sem.at[i], sends))
-    for r in state:
-        r.first = [r.send(r.planes(), k, 0, by) for k, by in enumerate((1, -1, 2))]
-    for r in state:
+    routes = [
+        Route(me, full, order, rows, send_sem.at[i], recv_sem.at[i], sends)
+        for i, (order, rows) in enumerate(colors)
+    ]
+    for r in routes:
+        r.first = [r.send(r.planes(), n, 0, by) for n, by in enumerate(WAYS)]
+    for r in routes:
         wait_all(r.first)
-        r.second = [r.send(r.planes(a=ALL), 3 + k, 1, by) for k, by in enumerate((1, -1))]
-        r.third = {0: r.outward(0)}
+        r.second = [r.send(r.planes(a=ALL), 3 + n, 1, by) for n, by in enumerate(WAYS)]
+    for r in routes:
+        r.outward(0)
     if meanwhile is not None:
         meanwhile()
-    for r in state:
-        r.second_far = []
-        for half, by in ((0, 1), (1, -1)):
-            r.second[half].wait_recv()
-            r.second_far.append(r.send(r.planes(a=half, b=-by), 5 + half, 1, by))
-            r.third[-by] = r.outward(-by)
-    for r in state:
+    for n, group in ((1, -1), (2, 1)):
+        for r in routes:
+            r.second[n].wait_recv()
+            r.outward(group)
+    for r in routes:
         r.pass_on(0)
-    for r in state:
-        wait_all(r.second_far)
-        r.third[2] = r.outward(2)
-    for group in (-1, 1, 2):
-        for r in state:
+    for r in routes:
+        r.second[0].wait_recv()
+        r.last += [r.send(r.planes(a=ALL, b=2), 6 + n, 2, by) for n, by in enumerate(WAYS)]
+    for group in (-1, 1):
+        for r in routes:
             r.pass_on(group)
-    for r in state:
+    for r in routes:
         wait_all(r.last)
     return sends
+
+
+WAYS = (2, 1, -1)
 
 
 def wait_all(copies):
@@ -123,17 +117,18 @@
     def __init__(self, me, ref, order, rows, send_sem, recv_sem, sends):
         self.me, self.ref, self.order, self.rows = me, ref, order, rows
         self.send_sem, self.recv_sem, self.sends = send_sem, recv_sem, sends
+        self.third = {}
         self.last = []
 
-    def planes(self, a=None, b=0, c=0):
+    def planes(self, a=0, b=0, c=0):
         me, (da, db, dc) = self.me, self.order
         spec = {db: me.step(db, b), dc: me.step(dc, c)}
-        if a is None:
-            spec[da] = me.at[da]
-        elif a is ALL:
+        if a is ALL:
             spec[da] = ALL
+        elif isinstance(a, tuple):
+            spec[da] = pl.ds(2 * a[0], 2)
         else:
-            spec[da] = pl.ds(2 * a, 2)
+            spec[da] = me.step(da, a)
         return self.ref.at[spec["x"], spec["z"], spec["y"], self.rows]
 
     def send(self, src, k, axis, by, dst=None):
@@ -148,109 +143,60 @@
         return copy
 
     def slot(self, group):
-        return 7 + 4 * (group % 4)
+        return 9 + 4 * (group % 4)
 
     def outward(self, group):
         k = self.slot(group)
-        return [self.send(self.planes(a=ALL, b=group), k + n, 2, by) for n, by in enumerate((1, -1))]
+        src = self.planes(a=ALL, b=group)
+        self.third[group] = [self.send(src, k + n, 2, by) for n, by in enumerate((1, -1))]
 
     def pass_on(self, group):
         k = self.slot(group) + 2
         for half, by in ((0, 1), (1, -1)):
             self.third[group][half].wait_recv()
-            self.last.append(self.send(self.planes(a=half, b=group, c=-by), k + half, 2, by))
+            self.last.append(self.send(self.planes(a=(half,), b=group, c=-by), k + half, 2, by))
 
 
 def landing_shapes(colors):
     shapes = []
-    for order, rows in colors:
-        for phase in (2, 1):
-            kept = [a for a in DIMS if a in order[:phase]]
-            lead = tuple(2 if a == order[0] else 4 for a in kept)
-            shapes.append(pltpu.VMEM((6, *lead, rows.size, L), F32))
+    for _, rows in colors:
+        shapes.append(pltpu.VMEM((4, 3, 4, rows.size, L), F32))
+        shapes.append(pltpu.VMEM((3, 4, rows.size, L), F32))
         shapes.append(pltpu.VMEM((3, rows.size, L), F32))
     return shapes
 
 
 def scatter_sums(me, part, landing, colors, send_sem, recv_sem):
     sends = []
-    for phase in (2, 1):
-        started = []
-        for c, (order, rows) in enumerate(colors):
-            axis = order[phase]
-            land = landing[3 * c + 2 - phase]
-            started.append(
-                [
-                    remote(
-                        me.region(part, order, phase, me.step(axis, 2), rows, half),
-                        land.at[half],
-                        send_sem.at[c, phase, half],
-                        recv_sem.at[c, phase, half],
-                        me.peer(axis, by),
-                    )
-                    for half, by in ((0, 1), (1, -1))
-                ]
-            )
-        for c, (order, rows) in enumerate(colors):
-            axis = order[phase]
-            land = landing[3 * c + 2 - phase]
-            for k, half, by in ((2, 1, 1), (3, 0, -1)):
-                started[c].append(
-                    remote(
-                        me.region(part, order, phase, me.step(axis, by), rows, half),
-                        land.at[k],
-                        send_sem.at[c, phase, k],
-                        recv_sem.at[c, phase, k],
-                        me.peer(axis, by),
-                    )
-                )
-        for c, (order, rows) in enumerate(colors):
-            axis = order[phase]
-            land = landing[3 * c + 2 - phase]
-            for k, half, by in ((4, 0, 1), (5, 1, -1)):
-                started[c][half].wait_recv()
-                onward = me.region(part, order, phase, me.step(axis, by), rows, half)
-                onward[...] = onward[...] + land[half]
-                started[c].append(
-                    remote(
-                        onward,
-                        land.at[k],
-                        send_sem.at[c, phase, k],
-                        recv_sem.at[c, phase, k],
-                        me.peer(axis, by),
-                    )
-                )
-        for c, (order, rows) in enumerate(colors):
-            axis = order[phase]
-            land = landing[3 * c + 2 - phase]
-            for copy in started[c][2:]:
-                copy.wait_recv()
-            for half, (one, other) in enumerate(((3, 4), (2, 5))):
-                mine = me.region(part, order, phase, me.at[axis], rows, half)
-                mine[...] = mine[...] + (land[one] + land[other])
-            sends += started[c]
-    started = []
-    for c, (order, rows) in enumerate(colors):
-        land = landing[3 * c + 2]
-        started.append(
-            [
-                remote(
-                    me.region(part, order, 0, me.step(order[0], by), rows),
-                    land.at[by - 1],
-                    send_sem.at[c, 0, by],
-                    recv_sem.at[c, 0, by],
-                    me.peer(order[0], by),
-                )
-                for by in (1, 2, 3)
+    routes = []
+    for i, (order, rows) in enumerate(colors):
+        r = Route(me, part, order, rows, send_sem.at[i], recv_sem.at[i], sends)
+        r.on_c, r.on_b, r.on_a = landing[3 * i : 3 * i + 3]
+        r.second = []
+        routes.append(r)
+    groups = (2, -1, 1, 0)
+    for g, group in enumerate(groups):
+        for r in routes:
+            r.third[group] = [
+                r.send(r.planes(a=ALL, b=group, c=by), 3 * g + n, 2, by, r.on_c.at[g, n])
+                for n, by in enumerate(WAYS)
             ]
-        )
-    for c, (order, rows) in enumerate(colors):
-        land = landing[3 * c + 2]
-        for copy in started[c]:
-            copy.wait_recv()
-        mine = me.region(part, order, 0, me.at[order[0]], rows)
-        mine[...] = mine[...] + ((land[0] + land[1]) + land[2])
-        sends += started[c]
+    for g, group in enumerate(groups):
+        for r in routes:
+            wait_all(r.third[group])
+            mine = r.planes(a=ALL, b=group)
+            mine[...] = (mine[...] + r.on_c[g, 0]) + (r.on_c[g, 1] + r.on_c[g, 2])
+            if group != 0:
+                r.second.append(r.send(mine, 12 + g, 1, group, r.on_b.at[g]))
+    for r in routes:
+        wait_all(r.second)
+        mine = r.planes(a=ALL)
+        mine[...] = (mine[...] + r.on_b[0]) + (r.on_b[1] + r.on_b[2])
+        r.first = [r.send(r.planes(a=by), 15 + n, 0, by, r.on_a.at[n]) for n, by in enumerate(WAYS)]
+    for r in routes:
+        wait_all(r.first)
+        mine = r.planes()
+        mine[...] = (mine[...] + r.on_a[0]) + (r.on_a[1] + r.on_a[2])
     return sends
 
 
@@ -301,7 +247,7 @@
     return upper, (values - upper.astype(F32)).astype(BF16)
 
 
-def respond(fields, dens, pot, shifts, kx, part, trial_lines):
+def respond(fields, dens, pot, shifts, kx, part, trial_lines, after_begin=None):
     u0, u1, u2, near_even, near_odd, stack_even, stack_odd = fields
     slots = range(dens.shape[0])
     lines = near_even.shape[1]
@@ -318,6 +264,8 @@
         return 0
 
     lax.fori_loop(0, G, begin, 0, unroll=4)
+    if after_begin is not None:
+        after_begin()
 
     def along_z(u, chunk, near):
         for k in range(lines):
@@ -416,6 +364,8 @@
     potential,
     coulomb,
     out,
+    orbital_lines,
+    orbital_sem,
     full,
     mapped,
     pot_other,
@@ -452,6 +402,8 @@
     for peer in peers:
         pl.semaphore_signal(barrier, inc=1, device_id=peer, device_id_type=MESH)
 
+    orbital_copy = pltpu.make_async_copy(orbitals, orbital_lines, orbital_sem)
+    orbital_copy.start()
     plane = me.own(full)
     for k in range(G // 2):
         a = trials[0, :, k * L : (k + 1) * L]
@@ -477,10 +429,11 @@
                 u[s, 0] = jnp.zeros((GROUP, L), F32)
                 u[s, G + 1] = jnp.zeros((GROUP, L), F32)
         lax.fori_loop(1, G + 1, clear, 0)
+        orbital_copy.wait()
 
         def spread_out(k, _):
             for s in slots:
-                t = orbitals[s, :, pl.ds(pl.multiple_of(k * L, L), L)].astype(F32)
+                t = orbital_lines[s, :, pl.ds(pl.multiple_of(k * L, L), L)].astype(F32)
                 turned = swap(t)
                 dens[s, 2 * k] = jnp.where(half, t, turned)
                 dens[s, 2 * k + 1] = jnp.where(half, turned, t)
@@ -511,9 +464,10 @@
         level(j, (1 - me.trial) * EXTRA, other_rows[pl.ds(j, G, stride=EXTRA), :])
         return 0
 
-    lax.fori_loop(0, EXTRA, own_level, 0)
-    pot_copy.wait_recv()
-    lax.fori_loop(0, EXTRA, other_level, 0)
+    def levels():
+        lax.fori_loop(0, EXTRA, own_level, 0, unroll=2)
+        pot_copy.wait_recv()
+        lax.fori_loop(0, EXTRA, other_level, 0, unroll=2)
 
     shifts = []
     for s in slots:
@@ -538,7 +492,14 @@
     fields = (u0, u1, u2, near_even, near_odd, stack_even, stack_odd)
     total = me.own(part)
     respond(
-        fields, dens, pot, shifts, kx_parts, part, lambda y: full_rows[pl.ds(y, G, stride=G + EXTRA), :]
+        fields,
+        dens,
+        pot,
+        shifts,
+        kx_parts,
+        part,
+        lambda y: full_rows[pl.ds(y, G, stride=G + EXTRA), :],
+        levels,
     )
     n = len(landing) // 2
     part_sends = scatter_sums(me, part, landing[:n], SUM_COLORS, sum_send.at[0], sum_recv.at[0])
@@ -673,9 +634,11 @@
     return pl.pallas_call(
         kernel,
         out_shape=jax.ShapeDtypeStruct(trials.shape, F32),
-        in_specs=[smem] * 4 + [vmem] * 4,
+        in_specs=[smem] * 4 + [vmem, pl.BlockSpec(memory_space=pl.ANY), vmem, vmem],
         out_specs=vmem,
         scratch_shapes=[
+            pltpu.VMEM(orbitals.shape, BF16),
+            dma,
             pltpu.VMEM((4, 4, 4, G + EXTRA, L), F32),
             pltpu.VMEM((4, 4, 4, G + SUMS, L), F32),
             pltpu.VMEM((4, 4, 4, EXTRA, L), F32),
@@ -691,12 +654,12 @@
             pltpu.VMEM((4, 4, 4, G, L), F32),
             pltpu.VMEM((3, G, L), F32),
             pltpu.VMEM((4, 4, 8, L), F32),
-            dma((3, 23)),
-            dma((3, 23)),
-            dma((3, 23)),
-            dma((3, 23)),
-            dma((2, 3, 3, 6)),
-            dma((2, 3, 3, 6)),
+            dma((3, 25)),
+            dma((3, 25)),
+            dma((3, 25)),
+            dma((3, 25)),
+            dma((2, 3, 18)),
+            dma((2, 3, 18)),
             dma((2,)),
             dma((2,)),
             dma((3, 4)),

time: 140 us -> 123 us (0.88)
  Pallas kernels: 138 us -> 122 us
    pallas_call x1, Pallas kernels: 138 us -> 122 us  [shards(): pl.pallas_call(kernel, out_shape=jax.ShapeDtypeStruct(trials.shape, F32),...]
where the time goes in v3:
time: 123 us
  Pallas kernels  122 us (99%)
  local copies, waits for them, and re-layouts  1.38 us (1%)
    pallas_call x1, Pallas kernels, shards(): pl.pallas_call(kernel, out_shape=jax.ShapeDtypeStruct(trials.shape, F32),...  122 us

profile of v3, /device:TPU:0, one launch (start us, length us, event | category | flops | bytes accessed | tf_op | source)
XLA Modules:
  0.0 123.1 jit_solution(6139071296332102406)
XLA Ops:
  0.0 121.7 %filter.1 = f32[2,1,4096]{2,1,0:T(1,128)} custom-call(f32[128]{0:T(128)} %energies.1, f32[8]{0:T(128)} %frequencies.1, s32[2]{0:T(128)} %orbital_ids.1, s32[2]{0:T(128)} %freq_index.1, f32[2,1,4096]{2,1,0:T(1,128)} %trials.1, bf16[2,64,4096]{2,1,0:T(8,128)(2,1)} %orbitals.1, f32[1,4096]{1,0:T(1,128)} %potential.1, f32[3,64,64]{2,1,0:T(8,128)} %coulomb.1), custom_call_target="tpu_custom_call" | custom-call | tf_op jit(solution)/shard_map/filter/pallas_call | solution.py:634
  121.7 1.4 %copy.10 = f32[2,1,4096]{2,1,0:T(1,128)} copy(f32[2,1,4096]{2,1,0:T(1,128)} %filter.1) | data formatting | bytes 65536

commit v4 on v3

--- a/solution.py
+++ b/solution.py
@@ -17,15 +17,16 @@
 STRIDE = {"x": 16, "z": 4, "y": 1}
 
 GROUP = 80
+WIDE = 4
 LINES = 8
 MID = 1.25
 EXTRA = 16
 SUMS = 8
 
 FIRST_COLORS = (
+    (("x", "y", "z"), pl.ds(56, 24)),
     (("y", "z", "x"), pl.ds(0, 32)),
     (("z", "x", "y"), pl.ds(32, 24)),
-    (("x", "y", "z"), pl.ds(56, 24)),
 )
 SECOND_COLORS = (
     (("y", "z", "x"), pl.ds(0, 24)),
@@ -73,7 +74,7 @@
     return copy
 
 
-def gather(me, full, colors, send_sem, recv_sem, meanwhile=None):
+def gather(me, full, colors, send_sem, recv_sem, meanwhile=None, done=None):
     sends = []
     routes = [
         Route(me, full, order, rows, send_sem.at[i], recv_sem.at[i], sends)
@@ -100,8 +101,10 @@
     for group in (-1, 1):
         for r in routes:
             r.pass_on(group)
-    for r in routes:
+    for i, r in enumerate(routes):
         wait_all(r.last)
+        if done is not None:
+            done(i)
     return sends
 
 
@@ -166,38 +169,46 @@
     return shapes
 
 
-def scatter_sums(me, part, landing, colors, send_sem, recv_sem):
-    sends = []
-    routes = []
-    for i, (order, rows) in enumerate(colors):
-        r = Route(me, part, order, rows, send_sem.at[i], recv_sem.at[i], sends)
-        r.on_c, r.on_b, r.on_a = landing[3 * i : 3 * i + 3]
-        r.second = []
-        routes.append(r)
-    groups = (2, -1, 1, 0)
-    for g, group in enumerate(groups):
-        for r in routes:
-            r.third[group] = [
-                r.send(r.planes(a=ALL, b=group, c=by), 3 * g + n, 2, by, r.on_c.at[g, n])
-                for n, by in enumerate(WAYS)
-            ]
-    for g, group in enumerate(groups):
-        for r in routes:
-            wait_all(r.third[group])
-            mine = r.planes(a=ALL, b=group)
-            mine[...] = (mine[...] + r.on_c[g, 0]) + (r.on_c[g, 1] + r.on_c[g, 2])
-            if group != 0:
-                r.second.append(r.send(mine, 12 + g, 1, group, r.on_b.at[g]))
-    for r in routes:
-        wait_all(r.second)
-        mine = r.planes(a=ALL)
-        mine[...] = (mine[...] + r.on_b[0]) + (r.on_b[1] + r.on_b[2])
-        r.first = [r.send(r.planes(a=by), 15 + n, 0, by, r.on_a.at[n]) for n, by in enumerate(WAYS)]
-    for r in routes:
-        wait_all(r.first)
-        mine = r.planes()
-        mine[...] = (mine[...] + r.on_a[0]) + (r.on_a[1] + r.on_a[2])
-    return sends
+GROUPS = (2, -1, 1, 0)
+
+
+class Scatter:
+    def __init__(self, me, part, landing, colors, send_sem, recv_sem):
+        self.sends = []
+        self.routes = []
+        for i, (order, rows) in enumerate(colors):
+            r = Route(me, part, order, rows, send_sem.at[i], recv_sem.at[i], self.sends)
+            r.on_c, r.on_b, r.on_a = landing[3 * i : 3 * i + 3]
+            r.second = []
+            self.routes.append(r)
+
+    def start(self, first_row):
+        for r in self.routes:
+            if r.rows.start == first_row:
+                for g, group in enumerate(GROUPS):
+                    r.third[group] = [
+                        r.send(r.planes(a=ALL, b=group, c=by), 3 * g + n, 2, by, r.on_c.at[g, n])
+                        for n, by in enumerate(WAYS)
+                    ]
+
+    def finish(self):
+        for g, group in enumerate(GROUPS):
+            for r in self.routes:
+                wait_all(r.third[group])
+                mine = r.planes(a=ALL, b=group)
+                mine[...] = (mine[...] + r.on_c[g, 0]) + (r.on_c[g, 1] + r.on_c[g, 2])
+                if group != 0:
+                    r.second.append(r.send(mine, 12 + g, 1, group, r.on_b.at[g]))
+        for r in self.routes:
+            wait_all(r.second)
+            mine = r.planes(a=ALL)
+            mine[...] = (mine[...] + r.on_b[0]) + (r.on_b[1] + r.on_b[2])
+            r.first = [r.send(r.planes(a=by), 15 + n, 0, by, r.on_a.at[n]) for n, by in enumerate(WAYS)]
+        for r in self.routes:
+            wait_all(r.first)
+            mine = r.planes()
+            mine[...] = (mine[...] + r.on_a[0]) + (r.on_a[1] + r.on_a[2])
+        return self.sends
 
 
 def lanes():
@@ -247,7 +258,7 @@
     return upper, (values - upper.astype(F32)).astype(BF16)
 
 
-def respond(fields, dens, pot, shifts, kx, part, trial_lines, after_begin=None):
+def respond(fields, dens, pot, shifts, kx, part, trial_lines, after_begin=None, bands=((0, G),), after_band=None):
     u0, u1, u2, near_even, near_odd, stack_even, stack_odd = fields
     slots = range(dens.shape[0])
     lines = near_even.shape[1]
@@ -324,34 +335,38 @@
         weights.append(step_weights(moments, shifts[s]))
 
     rows = part.reshape(G * G, L)
+    wide = stack_even.shape[1] // L
 
     def gathered(j, stack):
-        for k in range(2):
-            y = 2 * j + k
+        for k in range(wide):
+            y = wide * j + k
             total = None
             for s in slots:
                 w = [c * u[s, y + 1, 8:72] for c, u in zip(weights[s], (u0, u1, u2))]
                 term = (w[0] + w[1] + w[2]) * dens[s, y]
                 total = term if total is None else total + term
-            upper, lower = split(-total)
+            upper, lower = split(total)
             stack[0:G, k * L : k * L + L] = upper
             stack[G : 2 * G, k * L : k * L + L] = upper
             stack[2 * G : 3 * G, k * L : k * L + L] = lower
 
     def mixed(j, stack):
         sums = jnp.dot(kx, stack[...], preferred_element_type=F32)
-        for k in range(2):
-            rows[pl.ds(2 * j + k, G, stride=G), :] = sums[:, k * L : k * L + L]
+        for k in range(wide):
+            rows[pl.ds(wide * j + k, G, stride=G), :] = sums[:, k * L : k * L + L]
 
     gathered(0, stack_even)
 
     def finish(j, _):
-        for stack, ahead, y_pair in ((stack_even, stack_odd, 2 * j), (stack_odd, stack_even, 2 * j + 1)):
-            gathered(lax.rem(y_pair + 1, jnp.int32(G // 2)), ahead)
-            mixed(y_pair, stack)
+        for stack, ahead, at in ((stack_even, stack_odd, 2 * j), (stack_odd, stack_even, 2 * j + 1)):
+            gathered(lax.rem(at + 1, jnp.int32(G // wide)), ahead)
+            mixed(at, stack)
         return 0
 
-    lax.fori_loop(0, G // 4, finish, 0)
+    for start, stop in bands:
+        lax.fori_loop(start // (2 * wide), stop // (2 * wide), finish, 0)
+        if after_band is not None:
+            after_band(start)
 
 
 def kernel(
@@ -441,11 +456,6 @@
 
         lax.fori_loop(0, G // 2, spread_out, 0)
 
-    sends = gather(me, full, FIRST_COLORS, first_send, first_recv, prepare)
-
-    pot_lines = full.at[:, :, :, pl.ds(G, EXTRA)]
-    pot_copy = remote(pot_lines, pot_other, pair_send.at[0], pair_recv.at[0], me.partner())
-
     full_rows = full.reshape(G * (G + EXTRA), L)
     other_rows = pot_other.reshape(G * EXTRA, L)
     mapped_rows = mapped.reshape(G * (G + SUMS), L)
@@ -464,8 +474,18 @@
         level(j, (1 - me.trial) * EXTRA, other_rows[pl.ds(j, G, stride=EXTRA), :])
         return 0
 
+    pot_copies = []
+
+    def exchange_potential(color):
+        if color == 0:
+            lines = full.at[:, :, :, pl.ds(G, EXTRA)]
+            pot_copies.append(remote(lines, pot_other, pair_send.at[0], pair_recv.at[0], me.partner()))
+            lax.fori_loop(0, EXTRA, own_level, 0, unroll=2)
+
+    sends = gather(me, full, FIRST_COLORS, first_send, first_recv, prepare, exchange_potential)
+    (pot_copy,) = pot_copies
+
     def levels():
-        lax.fori_loop(0, EXTRA, own_level, 0, unroll=2)
         pot_copy.wait_recv()
         lax.fori_loop(0, EXTRA, other_level, 0, unroll=2)
 
@@ -477,7 +497,7 @@
     kx = coulomb[0]
     kx_upper = kx.astype(BF16)
     kx_lower = (kx - kx_upper.astype(F32)).astype(BF16)
-    kx_parts = jnp.concatenate([kx_upper, kx_lower, kx_upper], axis=1)
+    kx_parts = -jnp.concatenate([kx_upper, kx_lower, kx_upper], axis=1)
     kz = jnp.concatenate([coulomb[2], coulomb[2]], axis=1)
     kz = jnp.concatenate([kz, kz], axis=0)
     same = (lax.broadcasted_iota(jnp.int32, (L, L), 0) < G) == (lax.broadcasted_iota(jnp.int32, (L, L), 1) < G)
@@ -489,8 +509,11 @@
         )
         return jnp.dot(coulomb[1], turned, precision=HIGHEST, preferred_element_type=F32)
 
+    bands = [(rows.start, rows.start + rows.size) for _, rows in SUM_COLORS]
     fields = (u0, u1, u2, near_even, near_odd, stack_even, stack_odd)
     total = me.own(part)
+    n = len(landing) // 2
+    scatter = Scatter(me, part, landing[:n], SUM_COLORS, sum_send.at[0], sum_recv.at[0])
     respond(
         fields,
         dens,
@@ -500,9 +523,10 @@
         part,
         lambda y: full_rows[pl.ds(y, G, stride=G + EXTRA), :],
         levels,
+        bands,
+        scatter.start,
     )
-    n = len(landing) // 2
-    part_sends = scatter_sums(me, part, landing[:n], SUM_COLORS, sum_send.at[0], sum_recv.at[0])
+    part_sends = scatter.finish()
     own_mapped = in_plane(total[...])
     own_trials = plane[0:G, :]
     sums = me.own(mapped)
@@ -530,8 +554,9 @@
 
     for copy in part_sends:
         copy.wait_send()
-    respond(fields, dens, pot, shifts, kx_parts, part, first_lines)
-    part_sends = scatter_sums(me, part, landing[n:], SUM_COLORS, sum_send.at[1], sum_recv.at[1])
+    scatter = Scatter(me, part, landing[n:], SUM_COLORS, sum_send.at[1], sum_recv.at[1])
+    respond(fields, dens, pot, shifts, kx_parts, part, first_lines, None, bands, scatter.start)
+    part_sends = scatter.finish()
     own_first = (own_mapped - center * own_trials) * unspread
     second = 2.0 * (in_plane(total[...]) - center * own_first) * unspread - own_trials
 
@@ -630,7 +655,7 @@
     dma = pltpu.SemaphoreType.DMA
     field = pltpu.VMEM((slots, G + 2, GROUP, L), F32)
     near = pltpu.VMEM((slots, LINES, G, L), F32)
-    stack = pltpu.VMEM((3 * G, 2 * L), BF16)
+    stack = pltpu.VMEM((3 * G, WIDE * L), BF16)
     return pl.pallas_call(
         kernel,
         out_shape=jax.ShapeDtypeStruct(trials.shape, F32),

time: 123 us -> 118 us (0.959)
  Pallas kernels: 122 us -> 116 us
    pallas_call x1, Pallas kernels: 122 us -> 116 us  [shards(): pl.pallas_call(kernel, out_shape=jax.ShapeDtypeStruct(trials.shape, F32),...]
where the time goes in v4:
time: 118 us
  Pallas kernels  116 us (98%)
  local copies, waits for them, and re-layouts  1.38 us (1%)
    pallas_call x1, Pallas kernels, shards(): pl.pallas_call(kernel, out_shape=jax.ShapeDtypeStruct(trials.shape, F32),...  116 us

profile of v4, /device:TPU:0, one launch (start us, length us, event | category | flops | bytes accessed | tf_op | source)
XLA Modules:
  0.0 117.6 jit_solution(826250432412782169)
XLA Ops:
  0.0 116.3 %filter.1 = f32[2,1,4096]{2,1,0:T(1,128)} custom-call(f32[128]{0:T(128)} %energies.1, f32[8]{0:T(128)} %frequencies.1, s32[2]{0:T(128)} %orbital_ids.1, s32[2]{0:T(128)} %freq_index.1, f32[2,1,4096]{2,1,0:T(1,128)} %trials.1, bf16[2,64,4096]{2,1,0:T(8,128)(2,1)} %orbitals.1, f32[1,4096]{1,0:T(1,128)} %potential.1, f32[3,64,64]{2,1,0:T(8,128)} %coulomb.1), custom_call_target="tpu_custom_call" | custom-call | tf_op jit(solution)/shard_map/filter/pallas_call | solution.py:659
  116.3 1.4 %copy.10 = f32[2,1,4096]{2,1,0:T(1,128)} copy(f32[2,1,4096]{2,1,0:T(1,128)} %filter.1) | data formatting | bytes 65536

commit v5 on v4

--- a/solution.py
+++ b/solution.py
@@ -569,29 +569,37 @@
     b = jnp.where(is_first, theirs, second)
     turned_a = swap(a)
     turned_b = swap(b)
+    place = lanes() % G
+    row = jnp.zeros((1, L), F32)
     for k, product in enumerate((a * a, a * turned_a, b * b, b * turned_b, a * b, a * turned_b)):
-        small[0, 0, k : k + 1] = column(fold(product))
-    small[0, 0, 6:8] = jnp.zeros((2, L), F32)
+        row = jnp.where(place == k, halves(column(fold(product))), row)
+    small[me.orb] = row
     sends += part_sends + [pot_copy, swap_copy]
-    for phase, axis in enumerate(DIMS):
-        copies = [
-            remote(
-                small.at[phase, 0],
-                small.at[phase, by],
-                small_send.at[phase, by],
-                small_recv.at[phase, by],
-                me.peer(axis, by),
-            )
-            for by in (1, 2, 3)
-        ]
-        for copy in copies:
-            copy.wait_recv()
-        small[phase + 1, 0] = (small[phase, 0] + small[phase, 1]) + (small[phase, 2] + small[phase, 3])
-        sends += copies
-    block = small[3, 0] * (1.0 / float(G**3))
-
-    def entry(row, upper):
-        picked = jnp.where(half, 0.0, block[row : row + 1]) if upper else jnp.where(half, block[row : row + 1], 0.0)
+    everyone = small.shape[0]
+    mine = small.at[me.orb]
+
+    def tell(i, _):
+        remote(
+            mine, mine, small_send, small_recv, (lax.rem(me.orb + i, jnp.int32(everyone)), me.trial)
+        )
+        return 0
+
+    lax.fori_loop(1, everyone, tell, 0)
+    others = small.at[pl.ds(0, everyone - 1)]
+    told = pltpu.make_async_remote_copy(
+        src_ref=others,
+        dst_ref=others,
+        send_sem=small_send,
+        recv_sem=small_recv,
+        device_id=me.partner(),
+        device_id_type=MESH,
+    )
+    told.wait_recv()
+    sends.append(told)
+    block = jnp.sum(small[...], axis=0) * (1.0 / float(G**3))
+
+    def entry(k, upper):
+        picked = jnp.where(lanes() == (k + G if upper else k), block, 0.0)
         return jnp.sum(picked, axis=1, keepdims=True)
 
     gram = {
@@ -678,7 +686,7 @@
             stack,
             pltpu.VMEM((4, 4, 4, G, L), F32),
             pltpu.VMEM((3, G, L), F32),
-            pltpu.VMEM((4, 4, 8, L), F32),
+            pltpu.VMEM((G, 1, L), F32),
             dma((3, 25)),
             dma((3, 25)),
             dma((3, 25)),
@@ -687,8 +695,8 @@
             dma((2, 3, 18)),
             dma((2,)),
             dma((2,)),
-            dma((3, 4)),
-            dma((3, 4)),
+            dma,
+            dma,
             *landing_shapes(SUM_COLORS),
             *landing_shapes(SUM_COLORS),
         ],

time: 118 us -> 115 us (0.975); the launches traced: 118 us -> 113 us
  Pallas kernels: 116 us -> 112 us
    pallas_call x1, Pallas kernels: 116 us -> 112 us  [shards(): pl.pallas_call(kernel, out_shape=jax.ShapeDtypeStruct(trials.shape, F32),...]
where the time goes in v5:
time: 115 us; the launch traced here: 113 us
  Pallas kernels  112 us (97%)
  local copies, waits for them, and re-layouts  1.38 us (1%)
    pallas_call x1, Pallas kernels, shards(): pl.pallas_call(kernel, out_shape=jax.ShapeDtypeStruct(trials.shape, F32),...  112 us

profile of v5, /device:TPU:0, one launch (start us, length us, event | category | flops | bytes accessed | tf_op | source)
XLA Modules:
  0.0 113.3 jit_solution(8694301260244903938)
XLA Ops:
  0.0 111.9 %filter.1 = f32[2,1,4096]{2,1,0:T(1,128)} custom-call(f32[128]{0:T(128)} %energies.1, f32[8]{0:T(128)} %frequencies.1, s32[2]{0:T(128)} %orbital_ids.1, s32[2]{0:T(128)} %freq_index.1, f32[2,1,4096]{2,1,0:T(1,128)} %trials.1, bf16[2,64,4096]{2,1,0:T(8,128)(2,1)} %orbitals.1, f32[1,4096]{1,0:T(1,128)} %potential.1, f32[3,64,64]{2,1,0:T(8,128)} %coulomb.1), custom_call_target="tpu_custom_call" | custom-call | tf_op jit(solution)/shard_map/filter/pallas_call | solution.py:667
  111.9 1.4 %copy.10 = f32[2,1,4096]{2,1,0:T(1,128)} copy(f32[2,1,4096]{2,1,0:T(1,128)} %filter.1) | data formatting | bytes 65536

commit v6 on v5

--- a/solution.py
+++ b/solution.py
@@ -370,15 +370,23 @@
 
 
 def kernel(
+    energies_in,
+    frequencies_in,
+    orbital_ids_in,
+    freq_index_in,
+    trials_in,
+    orbitals,
+    potential_in,
+    coulomb_in,
+    out,
     energies,
     frequencies,
     orbital_ids,
     freq_index,
     trials,
-    orbitals,
     potential,
     coulomb,
-    out,
+    input_sem,
     orbital_lines,
     orbital_sem,
     full,
@@ -412,6 +420,22 @@
     slots = range(dens.shape[0])
     half = lanes() < G
 
+    inputs = [
+        pltpu.make_async_copy(src, dst, input_sem.at[i])
+        for i, (src, dst) in enumerate(
+            (
+                (trials_in, trials),
+                (potential_in, potential),
+                (coulomb_in, coulomb),
+                (energies_in, energies),
+                (frequencies_in, frequencies),
+                (orbital_ids_in, orbital_ids),
+                (freq_index_in, freq_index),
+            )
+        )
+    ]
+    for copy in inputs:
+        copy.start()
     barrier = pltpu.get_barrier_semaphore()
     peers = [me.peer(a, by) for a in DIMS for by in (1, 2, 3)] + [me.partner()]
     for peer in peers:
@@ -420,6 +444,8 @@
     orbital_copy = pltpu.make_async_copy(orbitals, orbital_lines, orbital_sem)
     orbital_copy.start()
     plane = me.own(full)
+    for copy in inputs[:2]:
+        copy.wait()
     for k in range(G // 2):
         a = trials[0, :, k * L : (k + 1) * L]
         b = trials[1, :, k * L : (k + 1) * L]
@@ -445,6 +471,8 @@
                 u[s, G + 1] = jnp.zeros((GROUP, L), F32)
         lax.fori_loop(1, G + 1, clear, 0)
         orbital_copy.wait()
+        for copy in inputs[2:]:
+            copy.wait()
 
         def spread_out(k, _):
             for s in slots:
@@ -659,7 +687,6 @@
 def shards(trials, orbitals, potential, coulomb, energies, frequencies, orbital_ids, freq_index):
     slots = orbitals.shape[0]
     vmem = pl.BlockSpec(memory_space=pltpu.VMEM)
-    smem = pl.BlockSpec(memory_space=pltpu.SMEM)
     dma = pltpu.SemaphoreType.DMA
     field = pltpu.VMEM((slots, G + 2, GROUP, L), F32)
     near = pltpu.VMEM((slots, LINES, G, L), F32)
@@ -667,9 +694,12 @@
     return pl.pallas_call(
         kernel,
         out_shape=jax.ShapeDtypeStruct(trials.shape, F32),
-        in_specs=[smem] * 4 + [vmem, pl.BlockSpec(memory_space=pl.ANY), vmem, vmem],
+        in_specs=[pl.BlockSpec(memory_space=pl.ANY)] * 8,
         out_specs=vmem,
         scratch_shapes=[
+            *(pltpu.SMEM(a.shape, a.dtype) for a in (energies, frequencies, orbital_ids, freq_index)),
+            *(pltpu.VMEM(a.shape, a.dtype) for a in (trials, potential, coulomb)),
+            dma((7,)),
             pltpu.VMEM(orbitals.shape, BF16),
             dma,
             pltpu.VMEM((4, 4, 4, G + EXTRA, L), F32),

time: 115 us -> 113 us (0.983)
  Pallas kernels: 112 us -> 110 us
    pallas_call x1, Pallas kernels: 112 us -> 110 us  [shards(): pl.pallas_call(kernel, out_shape=jax.ShapeDtypeStruct(trials.shape, F32),...]
where the time goes in v6:
time: 113 us; the launch traced here: 112 us
  Pallas kernels  110 us (97%)
  local copies, waits for them, and re-layouts  1.38 us (1%)
    pallas_call x1, Pallas kernels, shards(): pl.pallas_call(kernel, out_shape=jax.ShapeDtypeStruct(trials.shape, F32),...  110 us

profile of v6, /device:TPU:0, one launch (start us, length us, event | category | flops | bytes accessed | tf_op | source)
XLA Modules:
  0.0 111.8 jit_solution(10155913892251892639)
XLA Ops:
  0.0 110.4 %filter.1 = f32[2,1,4096]{2,1,0:T(1,128)} custom-call(f32[128]{0:T(128)} %energies_in.1, f32[8]{0:T(128)} %frequencies_in.1, s32[2]{0:T(128)} %orbital_ids_in.1, s32[2]{0:T(128)} %freq_index_in.1, f32[2,1,4096]{2,1,0:T(1,128)} %trials_in.1, bf16[2,64,4096]{2,1,0:T(8,128)(2,1)} %orbitals.1, f32[1,4096]{1,0:T(1,128)} %potential_in.1, f32[3,64,64]{2,1,0:T(8,128)} %coulomb_in.1), custom_call_target="tpu_custom_call" | custom-call | tf_op jit(solution)/shard_map/filter/pallas_call | solution.py:694
  110.4 1.4 %copy.10 = f32[2,1,4096]{2,1,0:T(1,128)} copy(f32[2,1,4096]{2,1,0:T(1,128)} %filter.1) | data formatting | bytes 65536

commit v7 on v6

--- a/solution.py
+++ b/solution.py
@@ -274,7 +274,7 @@
             u0[s, y + 1, 8:72] = v * dens[s, y]
         return 0
 
-    lax.fori_loop(0, G, begin, 0, unroll=4)
+    lax.fori_loop(0, G, begin, 0, unroll=8)
     if after_begin is not None:
         after_begin()
 
@@ -508,14 +508,14 @@
         if color == 0:
             lines = full.at[:, :, :, pl.ds(G, EXTRA)]
             pot_copies.append(remote(lines, pot_other, pair_send.at[0], pair_recv.at[0], me.partner()))
-            lax.fori_loop(0, EXTRA, own_level, 0, unroll=2)
+            lax.fori_loop(0, EXTRA, own_level, 0, unroll=4)
 
     sends = gather(me, full, FIRST_COLORS, first_send, first_recv, prepare, exchange_potential)
     (pot_copy,) = pot_copies
 
     def levels():
         pot_copy.wait_recv()
-        lax.fori_loop(0, EXTRA, other_level, 0, unroll=2)
+        lax.fori_loop(0, EXTRA, other_level, 0, unroll=4)
 
     shifts = []
     for s in slots:

time: 113 us -> 113 us (level)
  no operation moved by 1% of the time
where the time goes in v7:
time: 113 us; the launch traced here: 111 us
  Pallas kernels  110 us (97%)
  local copies, waits for them, and re-layouts  1.38 us (1%)
    pallas_call x1, Pallas kernels, shards(): pl.pallas_call(kernel, out_shape=jax.ShapeDtypeStruct(trials.shape, F32),...  110 us

profile of v7, /device:TPU:0, one launch (start us, length us, event | category | flops | bytes accessed | tf_op | source)
XLA Modules:
  0.0 111.4 jit_solution(5691726211683687448)
XLA Ops:
  0.0 110.0 %filter.1 = f32[2,1,4096]{2,1,0:T(1,128)} custom-call(f32[128]{0:T(128)} %energies_in.1, f32[8]{0:T(128)} %frequencies_in.1, s32[2]{0:T(128)} %orbital_ids_in.1, s32[2]{0:T(128)} %freq_index_in.1, f32[2,1,4096]{2,1,0:T(1,128)} %trials_in.1, bf16[2,64,4096]{2,1,0:T(8,128)(2,1)} %orbitals.1, f32[1,4096]{1,0:T(1,128)} %potential_in.1, f32[3,64,64]{2,1,0:T(8,128)} %coulomb_in.1), custom_call_target="tpu_custom_call" | custom-call | tf_op jit(solution)/shard_map/filter/pallas_call | solution.py:694
  110.0 1.4 %copy.10 = f32[2,1,4096]{2,1,0:T(1,128)} copy(f32[2,1,4096]{2,1,0:T(1,128)} %filter.1) | data formatting | bytes 65536
